TPU v7x, 128 devices: a whole 4x4x4 slice. The times are simulated.
128 devices in a mesh: dp: 2 (over x_hi), seq: 8 (over x_lo, z), tensor: 8 (over y, core).
Axes of the slice: x: 4 (x_hi: 2, x_lo: 2; x = x_hi * 2 + x_lo), y: 4, z: 4, core: 2. Of those that a mesh axis runs over, the one named last changes fastest.
Arguments:
- image_states: bfloat16 [2, 4096, 3072], P('dp', 'seq', 'tensor'), may hold values from -6 to 6
- text_states: bfloat16 [4, 512, 3072], P(None, 'seq', 'tensor'), may hold values from -6 to 6
- image_qkv: bfloat16 [3072, 3, 3072], P(None, None, 'tensor'), may hold values from -0.109375 to 0.109375
- text_qkv: bfloat16 [3072, 3, 3072], P(None, None, 'tensor'), may hold values from -0.109375 to 0.109375
- image_out: bfloat16 [3072, 3072], P('tensor'), may hold values from -0.109375 to 0.109375
- final_weight: bfloat16 [3072, 64], replicated, may hold values from -0.109375 to 0.109375
- query_gain: float32 [128], replicated, may hold values from 1.5 to 2.5
- key_gain: float32 [128], replicated, may hold values from 1.5 to 2.5
- modulation: float32 [10, 7, 3072], replicated, may hold values from -3 to 3
- latent: float32 [2, 4096, 64], P('dp', ('seq', 'tensor')), may hold values from -6 to 6
- old_velocity: bfloat16 [2, 4096, 64], P('dp', ('seq', 'tensor')), may hold values from -6 to 6
- rollout_noise: float32 [2, 4096, 64], P('dp', ('seq', 'tensor')), may hold values from -6 to 6
- group_ids: int32 [2], P('dp'), may hold values from 0 to 3
- text_lengths: int32 [4], replicated, may hold values from 128 to 512
- step_ids: int32 [2], P('dp'), may hold values from 0 to 9
Outputs:
- step_mean: float32 [2, 4096, 64], P('dp', ('seq', 'tensor'))
- log_ratio: float32 [2], P('dp')
All inputs are finite; a program needn't handle non-finite values.
Results may differ from a plain program's by a relative error of at most 0.0023.
Values may be sent and summed in bfloat16 or wider, within the bound.
A program may use at most 192 MiB of HBM per device.

v0:
```python
import math

import jax
import jax.numpy as jnp
from jax import lax
from jax.sharding import PartitionSpec as P

NORM_EPSILON = 1e-06
NOISE_LEVEL = 0.7


def sent_together(arrays, axis, dim, along):
    widths = [a.shape[along] for a in arrays]
    both = jnp.concatenate(arrays, axis=along)
    result = lax.all_gather(both, axis, axis=dim, tiled=True)
    return tuple(jnp.split(result, [sum(widths[:k]) for k in range(1, len(widths))], axis=along))


def from_everyone(value, axis):
    length = lax.axis_size(axis)
    return lax.all_to_all(
        jnp.broadcast_to(value[None], (length, *value.shape)), axis, 0, 0, tiled=True
    )


def taken_together(value, axis):
    return from_everyone(value, axis).sum(axis=0)


def layer_norm(values):
    row_mean = jnp.mean(values, axis=-1, keepdims=True)
    centred = values - row_mean
    row_var = jnp.mean(centred * centred, axis=-1, keepdims=True)
    return centred * lax.rsqrt(row_var + NORM_EPSILON)


def head_norm(values, gain_vector):
    mean_square = jnp.mean(values * values, axis=-1, keepdims=True)
    return (values * lax.rsqrt(mean_square + NORM_EPSILON) * gain_vector).astype(jnp.bfloat16)


def plan(step_values, total_steps):
    step_count = total_steps + 1.0
    flow_time = (total_steps - step_values.astype(jnp.float32)) / step_count
    step_delta = -1.0 / step_count
    noise_sigma = NOISE_LEVEL * jnp.sqrt(flow_time / (1.0 - flow_time))
    spread = noise_sigma * jnp.sqrt(1.0 / step_count)
    return (flow_time, step_delta, noise_sigma, spread)


def drift_mean(latent_state, velocity, flow_time, step_delta, noise_sigma):
    drift = velocity + noise_sigma * noise_sigma / (2.0 * flow_time) * (
        latent_state + (1.0 - flow_time) * velocity
    )
    return latent_state + drift * step_delta


def shards(
    image_states,
    text_states,
    image_qkv,
    text_qkv,
    image_out,
    final_weight,
    query_gain,
    key_gain,
    modulation,
    latent,
    old_velocity,
    rollout_noise,
    group_ids,
    text_lengths,
    step_ids,
):
    samples = image_states.shape[0]
    local_img = image_states.shape[1]
    local_txt = text_states.shape[1]
    prompts = text_states.shape[0]
    head_dim = query_gain.shape[0]
    model_width = image_qkv.shape[0]
    local_heads = image_qkv.shape[2] // head_dim
    total_steps = modulation.shape[0]
    row_count = local_img // lax.axis_size("tensor")
    tensor_slot = lax.axis_index("tensor")
    step_pick = (step_ids[:, None] == jnp.arange(total_steps, dtype=jnp.int32)[None, :]).astype(
        jnp.float32
    )
    modrows = jnp.dot(
        step_pick, modulation.reshape(total_steps, -1), preferred_element_type=jnp.float32
    ).reshape(samples, 7, model_width)
    group_pick = group_ids[:, None] == jnp.arange(prompts, dtype=jnp.int32)[None, :]
    text_local = (
        jnp.dot(
            group_pick.astype(jnp.bfloat16),
            text_states.reshape(prompts, -1),
            preferred_element_type=jnp.float32,
        )
        .astype(jnp.bfloat16)
        .reshape(samples, local_txt, -1)
    )
    lengths = jnp.sum(jnp.where(group_pick, text_lengths[None, :], 0), axis=1)
    image_full, text_full = sent_together((image_states, text_local), "tensor", 2, 1)
    image_f = image_full.astype(jnp.float32)
    normed_img = (
        layer_norm(image_f) * (1.0 + modrows[:, 1, None, :]) + modrows[:, 0, None, :]
    ).astype(jnp.bfloat16)
    normed_txt = (
        layer_norm(text_full.astype(jnp.float32)) * (1.0 + modrows[:, 4, None, :])
        + modrows[:, 3, None, :]
    ).astype(jnp.bfloat16)

    def project(normed, weight):
        projected = jnp.dot(
            normed.reshape(-1, model_width),
            weight.reshape(model_width, -1),
            preferred_element_type=jnp.float32,
        )
        return projected.reshape(samples, normed.shape[1], 3, local_heads, head_dim)

    qkv_img = project(normed_img, image_qkv)
    qkv_txt = project(normed_txt, text_qkv)
    queries = head_norm(qkv_img[:, :, 0], query_gain)
    key_rows = head_norm(
        jnp.concatenate([qkv_txt[:, :, 1], qkv_img[:, :, 1]], axis=1), key_gain
    ).reshape(samples, local_txt + local_img, -1)
    value_rows = (
        jnp.concatenate([qkv_txt[:, :, 2], qkv_img[:, :, 2]], axis=1)
        .astype(jnp.bfloat16)
        .reshape(samples, local_txt + local_img, -1)
    )
    text_pos = lax.axis_index("seq") * local_txt + jnp.arange(local_txt, dtype=jnp.int32)
    text_valid = text_pos[None, :] < lengths[:, None]
    key_valid = jnp.concatenate([text_valid, jnp.ones((samples, local_img), bool)], axis=1).astype(
        jnp.bfloat16
    )
    score_scale = 1.0 / math.sqrt(head_dim)
    key_piece = lax.all_gather(key_rows, "seq", axis=1, tiled=True).reshape(
        samples, -1, local_heads, head_dim
    )
    value_piece = lax.all_gather(value_rows, "seq", axis=1, tiled=True).reshape(
        samples, -1, local_heads, head_dim
    )
    valid_piece = lax.all_gather(key_valid, "seq", axis=1, tiled=True).astype(jnp.float32)
    scores = (
        jnp.einsum("sqhd,skhd->shqk", queries, key_piece, preferred_element_type=jnp.float32)
        * score_scale
    )
    weights = jnp.exp(scores) * valid_piece[:, None, None, :]
    denominator = jnp.sum(weights, axis=-1)
    numerator = jnp.einsum(
        "shqk,skhd->shqd",
        weights.astype(jnp.bfloat16),
        value_piece,
        preferred_element_type=jnp.float32,
    )
    numerator, denominator = (numerator, denominator)
    attended = (numerator / denominator[..., None]).astype(jnp.bfloat16)
    attended = jnp.transpose(attended, (2, 0, 1, 3)).reshape(
        local_img, samples, local_heads * head_dim
    )
    summed = lax.psum_scatter(
        jnp.einsum("tsk,kd->tsd", attended, image_out, preferred_element_type=jnp.float32).astype(
            jnp.bfloat16
        ),
        "tensor",
        scatter_dimension=0,
        tiled=True,
    ).astype(jnp.float32)
    summed = jnp.transpose(summed, (1, 0, 2))
    own_rows = lax.dynamic_slice_in_dim(image_f, tensor_slot * row_count, row_count, 1)
    resid = own_rows + modrows[:, 2, None, :] * summed
    final_normed = (
        layer_norm(resid) * (1.0 + modrows[:, 6, None, :]) + modrows[:, 5, None, :]
    ).astype(jnp.bfloat16)
    velocity = jnp.dot(
        final_normed.reshape(-1, model_width), final_weight, preferred_element_type=jnp.float32
    ).reshape(samples, row_count, -1)
    flow_time, step_delta, noise_sigma, spread = plan(step_ids, total_steps)
    flow_e = flow_time[:, None, None]
    sigma_e = noise_sigma[:, None, None]
    step_mean = drift_mean(latent, velocity, flow_e, step_delta, sigma_e)
    mean_old = drift_mean(latent, old_velocity.astype(jnp.float32), flow_e, step_delta, sigma_e)
    shifted = rollout_noise + (mean_old - step_mean) / spread[:, None, None]
    partial_ratio = jnp.sum(rollout_noise * rollout_noise - shifted * shifted, axis=(1, 2)) * 0.5
    ratio_total = taken_together(partial_ratio, ("seq", "tensor"))
    elements = latent.shape[1] * lax.axis_size("seq") * lax.axis_size("tensor") * latent.shape[2]
    return (step_mean, ratio_total / elements)


def solution(mesh):
    placed = (
        P("dp", "seq", "tensor"),
        P(None, "seq", "tensor"),
        P(None, None, "tensor"),
        P(None, None, "tensor"),
        P("tensor", None),
        P(),
        P(),
        P(),
        P(),
        P("dp", ("seq", "tensor"), None),
        P("dp", ("seq", "tensor"), None),
        P("dp", ("seq", "tensor"), None),
        P("dp"),
        P(),
        P("dp"),
    )
    return jax.shard_map(
        shards,
        mesh=mesh,
        in_specs=placed,
        out_specs=(P("dp", ("seq", "tensor"), None), P("dp")),
        check_vma=False,
    )
```

profile of v0, /device:TPU:1, one launch (start us, length us, event | category | flops | bytes accessed | tf_op | source)
XLA Modules:
  0.0 243.8 jit_solution(12354884498779905535)
XLA Ops:
  8.0 1.1 copy.81
  9.4 1.8 pad_maximum_fusion
  11.9 1.3 pad.9
  13.7 0.7 reshape.504
  14.3 10.1 %copy.55 = bf16[3072,3,384]{0,2,1:T(8,128)(2,1)} copy(bf16[3072,3,384]{2,0,1:T(8,128)(2,1)} %param.17) | data formatting | bytes 14155776 | tf_op args[2]
  24.4 10.0 %copy.56 = bf16[3072,3,384]{0,2,1:T(8,128)(2,1)} copy(bf16[3072,3,384]{2,0,1:T(8,128)(2,1)} %param.18) | data formatting | bytes 14155776 | tf_op args[3]
  35.0 9.3 %all-gather.4.cloned.1.call-done = bf16[1,576,3072]{2,1,0:T(8,128)(2,1)} async-done(((bf16[1,576,384]{2,1,0:T(8,128)(2,1)}), bf16[1,576,3072]{2,1,0:T(8,128)(2,1)}) %all-gather.4.cloned.1.call-update) | async-done | bytes 3538960 | tf_op jit(solution)/shard_map/all_gather | solution.py:15
  44.3 2.5 %convert_reduce_fusion = f32[512]{0:T(512)S(1)} fusion(bf16[1,576,3072]{2,1,0:T(8,128)(2,1)} %all-gather.4.cloned.1.call-done), kind=kLoop, calls=%fused_computation.6 | loop fusion | flops 3145216 | bytes 3147776 | tf_op jit(solution)/shard_map/reduce_sum | solution.py:31
  46.8 3.0 %multiply_reduce_fusion = f32[512]{0:T(512)S(1)} fusion(f32[512]{0:T(512)S(1)} %broadcast_multiply_fusion, bf16[1,576,3072]{2,1,0:T(8,128)(2,1)} %all-gather.4.cloned.1.call-done), kind=kLoop, calls=%fused_computation.5 | loop fusion | flops 6290944 | bytes 3149824 | tf_op jit(solution)/shard_map/reduce_sum | solution.py:33
  49.9 6.9 %fusion.13 = f32[1,512,3,3,128]{1,4,3,2,0:T(8,128)S(1)} fusion(bf16[3,3,128,3072]{3,2,1,0:T(8,128)(2,1)} %bitcast.163, f32[3072]{0:T(1024)S(1)} %bitcast.182, f32[3072]{0:T(1024)S(1)} %bitcast.181, f32[512]{0:T(512)S(1)} %add_rsqrt_fusion.2, f32[512]{0:T(512)S(1)} %broadcast_multiply_fusion, bf16[1,576,3072]{2,1,0:T(8,128)(2,1)S(1)} %copy-done.1), kind=kOutput, calls=%fused_computation.17 | convolution fusion | flops 3633315840 | bytes 12611584 | tf_op jit(solution)/shard_map/dot_general | solution.py:113
  57.5 2.1 convolution_bitcast_fusion
  60.8 1.0 copy.58
  61.8 1.2 slice.78
  63.0 0.9 slice.79
  64.3 0.8 pad_maximum_fusion.1
  65.2 0.7 dynamic-slice
  66.6 0.7 fusion.79
  68.2 31.4 %all-reduce.1 = bf16[4608]{0:T(1024)(128)(2,1)S(1)} all-reduce(bf16[4608]{0:T(1024)(128)(2,1)S(1)} %dynamic-update-slice), channel_id=1, replica_groups=mesh['dp'=2,'seq'=8,'tensor'=8] {'seq'}, use_global_device_ids=true, to_apply=%add.1 | all-reduce | flops 4608 | bytes 18432
  99.6 9.0 %all-gather.6.cloned.1.call-done = bf16[1,4608,384]{2,1,0:T(8,128)(2,1)} async-done(((bf16[1,576,384]{2,1,0:T(8,128)(2,1)}), bf16[1,4608,384]{2,1,0:T(8,128)(2,1)}) %all-gather.6.cloned.1.call-update) | async-done | bytes 3538960 | tf_op jit(solution)/shard_map/all_gather | solution.py:137
  108.6 5.8 %copy.59 = bf16[1,4608,384]{1,2,0:T(8,128)(2,1)} copy(bf16[1,4608,384]{2,1,0:T(8,128)(2,1)} %all-gather.6.cloned.1.call-done) | data formatting | bytes 7077888 | tf_op jit(solution)/shard_map/all_gather | solution.py:137
  114.4 14.3 %fusion = (f32[3,512]{1,0:T(4,128)S(1)}, f32[3,512,4608]{2,1,0:T(8,128)}) fusion(f32[4608]{0:T(1024)S(1)} %mul.323, bf16[4608,3,128]{0,2,1:T(8,128)(2,1)} %bitcast.161, f32[1,512,3,3,128]{1,4,3,2,0:T(8,128)} %copy-done.2, f32[128]{0:T(128)S(1)} %copy-done.4, f32[512,3]{0,1:T(4,128)S(1)} %add_rsqrt_fusion.1), kind=kOutput, calls=%fused_computation.1 | convolution fusion | flops 1833761280 | bytes 32668160 | tf_op jit(solution)/shard_map/sqhd,skhd->shqk/dot_general | solution.py:145
  128.7 27.4 %all-gather.8.cloned.1.call-done = bf16[1,4608,384]{2,1,0:T(8,128)(2,1)} async-done(((bf16[1,576,384]{2,1,0:T(8,128)(2,1)}), bf16[1,4608,384]{2,1,0:T(8,128)(2,1)}) %all-gather.8.cloned.1.call-update) | async-done | bytes 3538960 | tf_op jit(solution)/shard_map/all_gather | solution.py:140
  156.1 5.8 %copy.64 = bf16[1,4608,384]{1,2,0:T(8,128)(2,1)} copy(bf16[1,4608,384]{2,1,0:T(8,128)(2,1)} %all-gather.8.cloned.1.call-done) | data formatting | bytes 7077888 | tf_op jit(solution)/shard_map/all_gather | solution.py:140
  161.9 12.9 %fusion.21 = bf16[3,512,128]{1,2,0:T(8,128)(2,1)S(1)} fusion(bf16[4608,3,128]{0,2,1:T(8,128)(2,1)} %bitcast.162, f32[3,512,4608]{2,1,0:T(8,128)} %get-tuple-element.15, f32[4608]{0:T(1024)S(1)} %mul.323, f32[3,512]{1,0:T(4,128)S(1)} %get-tuple-element.14), kind=kOutput, calls=%fused_computation.22 | convolution fusion | flops 1833566208 | bytes 32268288 | tf_op jit(solution)/shard_map/shqk,skhd->shqd/dot_general | solution.py:150
  174.9 3.5 %fusion.4 = bf16[512,1,3072]{2,0,1:T(8,128)(2,1)} fusion(bf16[512,384]{0,1:T(8,128)(2,1)S(1)} %bitcast.169, bf16[384,3072]{1,0:T(8,128)(2,1)S(1)} %copy-done), kind=kOutput, calls=%fused_computation.8 | convolution fusion | flops 1209532416 | bytes 5898240 | tf_op jit(solution)/shard_map/tsk,kd->tsd/dot_general | solution.py:162
  178.6 5.4 %slice_convert_fusion = f32[1,512,3072]{2,1,0:T(8,128)} fusion(bf16[1,576,3072]{2,1,0:T(8,128)(2,1)} %all-gather.4.cloned.1.call-done), kind=kLoop, calls=%fused_computation.16 | loop fusion | flops 1572864 | bytes 9437184 | tf_op jit(solution)/shard_map/convert_element_type | solution.py:103
  184.0 27.1 %reduce-scatter.2.cloned.1.call-done = bf16[64,1,3072]{2,0,1:T(8,128)(2,1)} async-done(((bf16[512,1,3072]{2,0,1:T(8,128)(2,1)}), bf16[64,1,3072]{2,0,1:T(8,128)(2,1)}) %reduce-scatter.2.cloned.1.call-update) | async-done | bytes 393232 | tf_op jit(solution)/shard_map/reduce_scatter | solution.py:161
  211.1 1.5 fusion.55
  212.5 1.5 multiply_reduce_fusion.1
  214.1 2.9 %fusion.71 = (f32[]{:T(128)}, f32[1,64,64]{2,1,0:T(8,128)}) fusion(f32[1,64,64]{2,1,0:T(8,128)S(1)} %copy-done.7, f32[1,64,64]{2,1,0:T(8,128)S(1)} %copy-done.8, bf16[1,64,64]{2,1,0:T(8,128)(2,1)S(1)} %copy-done.9, f32[]{:T(128)} %bitcast.52, f32[]{:T(128)} %bitcast.50, f32[]{:T(128)} %bitcast.49, bf16[3072,64]{0,1:T(8,128)(2,1)S(1)} %copy-done.6, ...), kind=kOutput, calls=%fused_computation.80 | convolution fusion | flops 26820608 | bytes 1669640 | tf_op jit(solution)/shard_map/dot_general | solution.py:175
  217.6 17.2 %all_to_all.6 = f32[64,1,1]{2,1,0:T(1,128)S(1)} all-to-all(f32[64,1,1]{2,1,0:T(1,128)S(1)} %broadcast_in_dim.6), channel_id=1, replica_groups=mesh['dp'=2,'seq'=8,'tensor'=8] {'seq','tensor'}, dimensions={0} | all-to-all | bytes 512 | tf_op jit(solution)/shard_map/all_to_all | solution.py:21
  234.8 0.7 reduce_sum.119
  (67 shorter events, 4.7 us)
Async XLA Ops:
  7.2 167.7 %copy-start = (bf16[384,3072]{1,0:T(8,128)(2,1)S(1)}, bf16[384,3072]{1,0:T(8,128)(2,1)}, u32[]{:S(2)}) copy-start(bf16[384,3072]{1,0:T(8,128)(2,1)} %param.19) | copy-start | bytes 7077892
  7.2 37.1 %all-gather.4.cloned.1.call-start = ((), (), s32[]{:S(2)}) async-start(), calls=%async_computation.2 | async-start | bytes 3981312 | tf_op jit(solution)/shard_map/all_gather | solution.py:15
  11.2 97.4 %all-gather.6.cloned.1.call-start = ((), (), s32[]{:S(2)}) async-start(), calls=%async_computation.3 | async-start | bytes 3981312 | tf_op jit(solution)/shard_map/all_gather | solution.py:137
  24.4 10.0 %copy-start.5 = (f32[128]{0:T(128)S(1)}, f32[128]{0:T(128)}, u32[]{:S(2)}) copy-start(f32[128]{0:T(128)} %param.22) | copy-start | bytes 1540
  44.3 5.6 %copy-start.1 = (bf16[1,576,3072]{2,1,0:T(8,128)(2,1)S(1)}, bf16[1,576,3072]{2,1,0:T(8,128)(2,1)}, u32[]{:S(2)}) copy-start(bf16[1,576,3072]{2,1,0:T(8,128)(2,1)} %all-gather.4.cloned.1.call-done) | copy-start | bytes 10616836
  46.8 10.6 %slice-start = ((s8[7077888]{0:T(1024)(128)(4,1)}), s8[4194304]{0:T(1024)(128)(4,1)S(1)}, s32[]{:S(2)}) async-start(s8[7077888]{0:T(1024)(128)(4,1)} %bitcast.158), calls=%async_computation.6 | async-start | bytes 8388608
  49.8 7.6 %slice-start.1 = ((s8[7077888]{0:T(1024)(128)(4,1)}), s8[2883584]{0:T(1024)(128)(4,1)S(1)}, s32[]{:S(2)}) async-start(s8[7077888]{0:T(1024)(128)(4,1)} %bitcast.158), calls=%async_computation.7 | async-start | bytes 5767168
  56.8 2.9 %copy-start.2 = (f32[1,512,3,3,128]{1,4,3,2,0:T(8,128)}, f32[1,512,3,3,128]{1,4,3,2,0:T(8,128)S(1)}, u32[]{:S(2)}) copy-start(f32[1,512,3,3,128]{1,4,3,2,0:T(8,128)S(1)} %fusion.13) | copy-start | bytes 7077892
  57.4 7.8 %copy-start.11 = (u32[128]{0:T(128)S(1)}, u32[128]{0:T(128)}, u32[]{:S(2)}) copy-start(u32[128]{0:T(128)} %constant.78) | copy-start | bytes 1540
  57.4 9.1 %copy-start.10 = (s32[4]{0:T(128)S(1)}, s32[4]{0:T(128)}, u32[]{:S(2)}) copy-start(s32[4]{0:T(128)} %param.28) | copy-start | bytes 52
  59.6 0.8 copy-start.3
  60.4 54.0 %copy-start.4 = (f32[128]{0:T(128)S(1)}, f32[128]{0:T(128)}, u32[]{:S(2)}) copy-start(f32[128]{0:T(128)} %param.21) | copy-start | bytes 1540
  61.8 94.3 %all-gather.8.cloned.1.call-start = ((), (), s32[]{:S(2)}) async-start(), calls=%async_computation.4 | async-start | bytes 3981312 | tf_op jit(solution)/shard_map/all_gather | solution.py:140
  65.1 145.9 %reduce-scatter.2.cloned.1.call-start = ((), (), s32[]{:S(2)}) async-start(), calls=%async_computation.5 | async-start | bytes 3538944 | tf_op jit(solution)/shard_map/reduce_scatter | solution.py:161
  178.4 35.7 %copy-start.6 = (bf16[3072,64]{0,1:T(8,128)(2,1)S(1)}, bf16[3072,64]{0,1:T(8,128)(2,1)}, u32[]{:S(2)}) copy-start(bf16[3072,64]{0,1:T(8,128)(2,1)} %param.20) | copy-start | bytes 1179652
  178.4 35.7 %copy-start.7 = (f32[1,64,64]{2,1,0:T(8,128)S(1)}, f32[1,64,64]{2,1,0:T(8,128)}, u32[]{:S(2)}) copy-start(f32[1,64,64]{2,1,0:T(8,128)} %param.26) | copy-start | bytes 49156
  178.4 35.7 %copy-start.8 = (f32[1,64,64]{2,1,0:T(8,128)S(1)}, f32[1,64,64]{2,1,0:T(8,128)}, u32[]{:S(2)}) copy-start(f32[1,64,64]{2,1,0:T(8,128)} %param.24) | copy-start | bytes 49156
  178.5 35.7 %copy-start.9 = (bf16[1,64,64]{2,1,0:T(8,128)(2,1)S(1)}, bf16[1,64,64]{2,1,0:T(8,128)(2,1)}, u32[]{:S(2)}) copy-start(bf16[1,64,64]{2,1,0:T(8,128)(2,1)} %param.25) | copy-start | bytes 24580
Sparse Core Ops, SparseCore 0:
  11.4 32.8 all-gather.3
  61.9 46.6 all-gather.5
  110.2 45.8 all-gather.7
  178.5 32.4 reduce-scatter.1
where the time goes:
time: 245 us; the launch traced here: 244 us
  waiting for transfers between devices  72.8 us (30%)
  blocking collectives  48.6 us (20%)
  matrix products  43.5 us (18%)
  local copies, waits for them, and re-layouts  40 us (16%)
  other arithmetic  19.9 us (8%)
  between operations  18.8 us (8%)
    unnamed x1, blocking collectives  31.4 us
    all_gather x1, waiting for transfers between devices, shards(): lax.all_gather(value_rows, 'seq', axis=1, tiled=True)  27.4 us
    reduce_scatter x1, waiting for transfers between devices, shards(): lax.psum_scatter(jnp.einsum('tsk,kd->tsd', attended, image_out, preferred...  27.1 us
    unnamed x36, local copies, waits for them, and re-layouts  24.2 us
    all_to_all x1, blocking collectives, from_everyone(): lax.all_to_all(jnp.broadcast_to(value[None], (length, *value.shape)), axi...  17.2 us
    dot_general x1, matrix products, shards(): jnp.einsum('sqhd,skhd->shqk', queries, key_piece, preferred_element_type=...  14.3 us
    dot_general x1, matrix products, shards(): jnp.einsum('shqk,skhd->shqd', weights.astype(jnp.bfloat16), value_piece,...  12.9 us
    all_gather x1, waiting for transfers between devices, sent_together(): result = lax.all_gather(both, axis, axis=dim, tiled=True)  9.28 us
  transfers between devices with their start and end apart: 4, of which 4 were waited for; matrix products, arithmetic and copies ran while one was open for 22% of the time, Pallas kernels for 0%

commit v1 on v0

v1 whole, which is shorter than its diff:
```python
import functools
import math

import jax
import jax.numpy as jnp
from jax import lax
from jax.experimental import pallas as pl
from jax.experimental.pallas import tpu as pltpu
from jax.sharding import PartitionSpec as P

NORM_EPSILON = 1e-06
NOISE_LEVEL = 0.7
F32 = jnp.float32
BF16 = jnp.bfloat16

TXT, IMG, TOK = 64, 512, 576
FEAT, PAIR, WIDTH = 384, 768, 3072
HEADS, HD = 3, 128
CH = 64
RING = 4
PARTS = ((0, 256), (256, 320))
VROWS = HD + 16
PAD = 640


def remote(src, dst, send, recv, where):
    return pltpu.make_async_remote_copy(
        src_ref=src,
        dst_ref=dst,
        send_sem=send,
        recv_sem=recv,
        device_id=where,
        device_id_type=pl.DeviceIdType.MESH,
    )


def piece(part, sub):
    start, rows = PARTS[part]
    return pl.ds(start + sub * (rows // 2), rows // 2)


def block(
    step_ref,
    group_ref,
    length_ref,
    x_ref,
    text_ref,
    wi_hbm,
    wt_hbm,
    wo_hbm,
    fw_ref,
    qg_ref,
    kg_ref,
    mod_ref,
    lat_ref,
    old_ref,
    noise_ref,
    mean_ref,
    ratio_ref,
    wi,
    wt,
    wo,
    xg,
    modv,
    st_col,
    st_all,
    stat,
    acc,
    qall,
    kv,
    oacc,
    osend,
    orecv,
    atts,
    attb,
    pso,
    pdir,
    pacc,
    pown,
    ropp,
    rdir,
    racc,
    rat1,
    rat2,
    w_sem,
    st_s,
    st_r,
    own_s,
    own_r,
    y_s,
    y_r,
    l_s,
    l_r,
    z_s,
    z_r,
    q_s,
    q_r,
    o_s,
    o_r,
    a_s,
    a_r,
    wo_s,
    wo_r,
    p_s,
    p_r,
    r1_s,
    r1_r,
    r2_s,
    r2_r,
):
    t = lax.axis_index("tensor")
    s = lax.axis_index("seq")
    y, c = lax.div(t, 2), lax.rem(t, 2)
    xlo, z = lax.div(s, RING), lax.rem(s, RING)
    yp, ym, yo = lax.rem(y + 1, RING), lax.rem(y + 3, RING), lax.rem(y + 2, RING)
    zp, zm, zo = lax.rem(z + 1, RING), lax.rem(z + 3, RING), lax.rem(z + 2, RING)
    mate = {"tensor": y * 2 + (1 - c)}
    y_dev = ({"tensor": yp * 2 + c}, {"tensor": ym * 2 + c})
    z_dev = ({"seq": xlo * RING + zp}, {"seq": xlo * RING + zm})
    x_dev = {"seq": (1 - xlo) * RING + z}
    cols = pl.ds(pl.multiple_of(c * FEAT, 128), FEAT)
    mate_cols = pl.ds(pl.multiple_of((1 - c) * FEAT, 128), FEAT)

    loads = []
    for j in range(3):
        loads.append(
            pltpu.make_async_copy(wi_hbm.at[j], wi.at[:, pl.ds(j * FEAT, FEAT)], w_sem.at[j])
        )
        loads.append(
            pltpu.make_async_copy(wt_hbm.at[j], wt.at[:, pl.ds(j * FEAT, FEAT)], w_sem.at[3 + j])
        )
    my_wo = wo.at[pl.ds(pl.multiple_of(c * FEAT, 128), FEAT)]
    wo_load = pltpu.make_async_copy(wo_hbm, my_wo, w_sem.at[6])
    for copy in loads:
        copy.start()
    wo_load.start()

    barrier = pltpu.get_barrier_semaphore()
    for j in range(1, 8):
        pl.semaphore_signal(
            barrier,
            inc=1,
            device_id={"tensor": lax.rem(t + j, 8)},
            device_id_type=pl.DeviceIdType.MESH,
        )
        pl.semaphore_signal(
            barrier,
            inc=1,
            device_id={"seq": lax.rem(s + j, 8)},
            device_id_type=pl.DeviceIdType.MESH,
        )

    group = group_ref[0]
    step = step_ref[0]
    xg[y, pl.ds(0, TXT), cols] = text_ref[group]
    xg[y, pl.ds(TXT, IMG), cols] = x_ref[0]

    mine = xg[y, :, cols].astype(F32)
    part_mean = jnp.mean(mine, axis=-1, keepdims=True)
    centred = mine - part_mean
    part_sq = jnp.sum(centred * centred, axis=-1, keepdims=True)
    lane = lax.broadcasted_iota(jnp.int32, (TOK, 128), 1)
    st_col[pl.ds(0, TOK), :] = jnp.where(lane == 0, part_mean, jnp.where(lane == 1, part_sq, 0.0))
    st_col[pl.ds(TOK, PAD - TOK), :] = jnp.zeros((PAD - TOK, 128), F32)
    st_all[t] = st_col[...].T[0:8, :]

    for i in range(RING):
        modv[i, pl.ds(0, 7), :] = mod_ref[step, :, pl.ds(i * PAIR, PAIR)]

    pl.semaphore_wait(barrier, 14)

    def peer_copy(buf, send, recv, axis, me, j):
        slot = buf.at[me]
        return remote(slot, slot, send.at[j], recv.at[j], {axis: lax.rem(me + j, 8)})

    def peer_arrival(buf, send, recv, axis, me, j):
        slot = buf.at[lax.rem(me + 8 - j, 8)]
        return remote(slot, slot, send.at[j], recv.at[j], {axis: lax.rem(me + j, 8)})

    stat_sends = [peer_copy(st_all, st_s, st_r, "tensor", t, j) for j in range(1, 8)]
    for copy in stat_sends:
        copy.start()

    def y_slot(d, k, sending):
        if k < 2:
            return (y if sending else (ym, yp)[d]), (k if d == 0 else 1 - k)
        return ((ym, yp)[d] if sending else yo), d

    def y_send(d, part, k):
        slot, sub = y_slot(d, k, True)
        ref = xg.at[slot, piece(part, sub), cols]
        return remote(ref, ref, y_s.at[d, part, k], y_r.at[d, part, k], y_dev[d])

    def y_arrival(d, part, k):
        slot, sub = y_slot(d, k, False)
        ref = xg.at[slot, piece(part, sub), cols]
        return remote(ref, ref, y_s.at[d, part, k], y_r.at[d, part, k], y_dev[d])

    def relay(d, part, k):
        slot, sub = y_slot(d, k, False)
        ref = xg.at[slot, piece(part, sub), cols]
        return remote(ref, ref, l_s.at[d, part, k], l_r.at[d, part, k], mate)

    def relay_arrival(d, part, k):
        slot, sub = y_slot(d, k, False)
        ref = xg.at[slot, piece(part, sub), mate_cols]
        return remote(ref, ref, l_s.at[d, part, k], l_r.at[d, part, k], mate)

    def own_copy(part, columns):
        ref = xg.at[y, pl.ds(*PARTS[part]), columns]
        return remote(ref, ref, own_s.at[part], own_r.at[part], mate)

    sends = list(stat_sends)

    def go(copy):
        copy.start()
        sends.append(copy)

    def y_own(part):
        for k in range(2):
            for d in range(2):
                go(y_send(d, part, k))

    y_own(0)
    go(own_copy(0, cols))
    go(own_copy(1, cols))

    for j in range(1, 8):
        peer_arrival(st_all, st_s, st_r, "tensor", t, j).wait_recv()
    means = st_all[:, 0, :]
    squares = st_all[:, 1, :]
    mean = jnp.mean(means, axis=0, keepdims=True)
    off = means - mean
    total_sq = jnp.sum(squares, axis=0, keepdims=True) + FEAT * jnp.sum(
        off * off, axis=0, keepdims=True
    )
    scale = lax.rsqrt(total_sq * (1.0 / WIDTH) + NORM_EPSILON)
    sub_row = lax.broadcasted_iota(jnp.int32, (128, PAD), 0)
    stat[...] = jnp.where(sub_row == 0, mean, jnp.where(sub_row == 1, scale, 0.0)).T

    for copy in loads:
        copy.wait()

    def project_rows(slot, start, rows, weight, shift_row, scale_row, first):
        at = pl.ds(start, rows)
        v = xg[slot, at, :].astype(F32)
        n = (v - stat[at, 0:1]) * stat[at, 1:2]
        n = n * (1.0 + modv[slot, pl.ds(scale_row, 1), :]) + modv[slot, pl.ds(shift_row, 1), :]
        w = weight[pl.ds(pl.multiple_of(slot * PAIR, 128), PAIR), :]
        p = jnp.dot(n.astype(BF16), w, preferred_element_type=F32)
        if first:
            acc[at, :] = p
        else:
            acc[at, :] += p

    def project(slot, part, first=False):
        start, rows = PARTS[part]
        if part == 0:
            project_rows(slot, TXT, rows - TXT, wi, 0, 1, first)
            project_rows(slot, 0, TXT, wt, 3, 4, first)
        else:
            project_rows(slot, start, rows, wi, 0, 1, first)

    score_scale = math.log2(math.e) / math.sqrt(HD)

    def head_norm(values, gain):
        square = jnp.mean(values * values, axis=-1, keepdims=True)
        return (values * lax.rsqrt(square + NORM_EPSILON) * gain).astype(BF16)

    def finish(part):
        start, rows = PARTS[part]
        at = pl.ds(start, rows)
        for h in range(HEADS):
            keys = acc[at, pl.ds(FEAT + h * HD, HD)]
            kv[z, at, pl.ds(h * HD, HD)] = head_norm(keys, kg_ref[...])
        kv[z, at, pl.ds(FEAT, FEAT)] = acc[at, pl.ds(2 * FEAT, FEAT)].astype(BF16)
        first = max(start, TXT)
        img = pl.ds(first, start + rows - first)
        for h in range(HEADS):
            query = acc[img, pl.ds(h * HD, HD)]
            qall[0, pl.ds(first - TXT, start + rows - first), pl.ds(h * HD, HD)] = head_norm(
                query, qg_ref[...] * score_scale
            )

    def z_slot(d, k, sending):
        if k < 2:
            return (z if sending else (zm, zp)[d]), (k if d == 0 else 1 - k)
        return ((zm, zp)[d] if sending else zo), d

    def z_send(d, part, k):
        slot, sub = z_slot(d, k, True)
        ref = kv.at[slot, piece(part, sub)]
        return remote(ref, ref, z_s.at[d, part, k], z_r.at[d, part, k], z_dev[d])

    def z_arrival(d, part, k):
        slot, sub = z_slot(d, k, False)
        ref = kv.at[slot, piece(part, sub)]
        return remote(ref, ref, z_s.at[d, part, k], z_r.at[d, part, k], z_dev[d])

    def q_copy(part):
        start, rows = PARTS[part]
        first = max(start, TXT)
        at = pl.ds(first - TXT, start + rows - first)
        return remote(qall.at[0, at], qall.at[1, at], q_s.at[part], q_r.at[part], x_dev)

    def z_own(part):
        for k in range(2):
            for d in range(2):
                go(z_send(d, part, k))

    for part in range(2):
        own_copy(part, mate_cols).wait_recv()
        project(y, part, first=True)
        for d in range(2):
            y_arrival(d, part, 0).wait_recv()
            go(y_send(d, part, 2))
            go(relay(d, part, 0))
        if part == 0:
            y_own(1)
        for d in range(2):
            y_arrival(d, part, 1).wait_recv()
            go(relay(d, part, 1))
        for k in range(2):
            for d in range(2):
                relay_arrival(d, part, k).wait_recv()
        project(ym, part)
        project(yp, part)
        for d in range(2):
            y_arrival(d, part, 2).wait_recv()
            go(relay(d, part, 2))
        for d in range(2):
            relay_arrival(d, part, 2).wait_recv()
        project(yo, part)
        finish(part)
        if part == 0:
            z_own(0)
        go(q_copy(part))

    wo_load.wait()
    wo_send = remote(my_wo, my_wo, wo_s.at[0], wo_r.at[0], mate)
    go(wo_send)

    length = length_ref[group]

    def attend(slot, part, sets, first=False):
        start, rows = PARTS[part]
        at = pl.ds(start, rows)

        def one_head(h, carry):
            at_k = pl.ds(pl.multiple_of(h * HD, 128), HD)
            at_v = pl.ds(pl.multiple_of(FEAT + h * HD, 128), HD)
            keys = kv[slot, at, at_k]
            vals = kv[slot, at, at_v].astype(F32).T
            ones = jnp.ones((VROWS - HD, rows), F32)
            if part == 0:
                pos = lax.broadcasted_iota(jnp.int32, (1, rows), 1)
                used = (pos >= TXT) | (pos + (xlo * RING + slot) * TXT < length)
                vals = jnp.where(used, vals, 0.0)
                ones = jnp.where(used, ones, 0.0)
            ext = jnp.concatenate([vals, ones], axis=0).astype(BF16)
            for q in sets:
                scores = lax.dot_general(
                    keys,
                    qall[q, :, at_k],
                    (((1,), (1,)), ((), ())),
                    preferred_element_type=F32,
                )
                e = jnp.exp2(scores).astype(BF16)
                o = jnp.dot(ext, e, preferred_element_type=F32)
                if first:
                    oacc[q, h] = o
                else:
                    oacc[q, h] += o
            return carry

        lax.fori_loop(0, HEADS, one_head, 0)

    for part in range(2):
        for d in range(2):
            z_arrival(d, part, 0).wait_recv()
            go(z_send(d, part, 2))
        if part == 0:
            z_own(1)
            q_wait = [q_copy(0), q_copy(1)]
            for copy in q_wait:
                copy.wait_recv()
            attend(z, 0, (1, 0), first=True)
            attend(z, 1, (1, 0))
        for d in range(2):
            z_arrival(d, part, 1).wait_recv()
        attend(zm, part, (1, 0))
        attend(zp, part, (1, 0))
        for d in range(2):
            z_arrival(d, part, 2).wait_recv()
        if part == 0:
            attend(zo, part, (1, 0))
    attend(zo, 1, (1,))

    order = (yo, yp, ym, y)

    def o_copy(j):
        return remote(osend.at[j], orecv.at[j], o_s.at[j], o_r.at[j], x_dev)

    def lanes(i):
        return pl.ds(pl.multiple_of(i * 128, 128), 128)

    for j in range(RING):
        at = lanes(order[j])
        for h in range(HEADS):
            osend[j, pl.ds(h * HD, HD), :] = oacc[1, h, pl.ds(0, HD), at].astype(BF16)
        whole = jnp.concatenate([oacc[1, h, pl.ds(HD, 1), at] for h in range(HEADS)], axis=0)
        high = whole.astype(BF16)
        rest = whole - high.astype(F32)
        middle = rest.astype(BF16)
        low = (rest - middle.astype(F32)).astype(BF16)
        osend[j, pl.ds(FEAT, 16), :] = jnp.concatenate(
            [high.astype(F32), middle.astype(F32), low.astype(F32), jnp.zeros((7, 128), F32)],
            axis=0,
        ).astype(BF16)
        go(o_copy(j))
    attend(zo, 1, (0,))

    def a_copy(j, columns):
        return remote(
            atts.at[j, pl.ds(pl.multiple_of((1 - c) * CH, CH), CH)],
            attb.at[j, :, columns],
            a_s.at[j],
            a_r.at[j],
            mate,
        )

    def combine(j):
        at = lanes(order[j])
        o_copy(j).wait_recv()
        tail = orecv[j, pl.ds(FEAT, 16), :].astype(F32)
        heads = []
        for h in range(HEADS):
            num = oacc[0, h, pl.ds(0, HD), at] + orecv[j, pl.ds(h * HD, HD), :].astype(F32)
            den = oacc[0, h, pl.ds(HD, 1), at] + (
                tail[h : h + 1] + tail[3 + h : 4 + h] + tail[6 + h : 7 + h]
            )
            heads.append((num / den).T)
        atts[j] = jnp.concatenate(heads, axis=1).astype(BF16)
        go(a_copy(j, cols))
        attb[j, :, cols] = atts[j, pl.ds(pl.multiple_of(c * CH, CH), CH), :]

    half = WIDTH // 2
    sides = (pl.ds(0, half), pl.ds(half, half))

    def p_copy(d, k):
        src = (pso.at[d], pdir.at[d], pacc.at[d])[k]
        dst = (ropp.at[d], rdir.at[d], racc.at[d])[k]
        return remote(src, dst, p_s.at[d, k], p_r.at[d, k], y_dev[d])

    def out_rows(j):
        a_copy(j, mate_cols).wait_recv()
        return jnp.dot(attb[j], wo[...], preferred_element_type=F32)

    def dispatch(j):
        p = out_rows(j)
        if j == 0:
            for d in range(2):
                pso[d] = p[:, d * half : (d + 1) * half].astype(BF16)
                go(p_copy(d, 0))
        elif j < 3:
            d = j - 1
            keep, direct = d, 1 - d
            pdir[d] = p[:, direct * half : (direct + 1) * half].astype(BF16)
            go(p_copy(d, 1))
            pown[:, sides[keep]] = p[:, keep * half : (keep + 1) * half]

    remote(my_wo, wo.at[pl.ds(pl.multiple_of((1 - c) * FEAT, 128), FEAT)], wo_s.at[0], wo_r.at[0], mate).wait_recv()
    for j in range(RING):
        combine(j)
        if j >= 1:
            dispatch(j - 1)
    last = out_rows(3)
    for d in range(2):
        p_copy(d, 0).wait_recv()
        pacc[d] = (pown[:, sides[d]] + ropp[d].astype(F32)).astype(BF16)
        go(p_copy(d, 2))
    pown[...] = last
    for d in range(2):
        p_copy(d, 1).wait_recv()
        pown[:, sides[1 - d]] += rdir[d].astype(F32)
    for d in range(2):
        p_copy(d, 2).wait_recv()
        pown[:, sides[d]] += racc[d].astype(F32)

    rows = pl.ds(pl.multiple_of(TXT + t * CH, CH), CH)
    resid = jnp.concatenate(
        [
            xg[i, rows, :].astype(F32)
            + modv[i, pl.ds(2, 1), :] * pown[:, pl.ds(i * PAIR, PAIR)]
            for i in range(RING)
        ],
        axis=1,
    )
    row_mean = jnp.mean(resid, axis=-1, keepdims=True)
    resid = resid - row_mean
    row_var = jnp.mean(resid * resid, axis=-1, keepdims=True)
    resid = resid * lax.rsqrt(row_var + NORM_EPSILON)
    velocity = jnp.zeros((CH, CH), F32)
    for i in range(RING):
        n = resid[:, i * PAIR : (i + 1) * PAIR] * (1.0 + modv[i, pl.ds(6, 1), :]) + modv[
            i, pl.ds(5, 1), :
        ]
        velocity += lax.dot_general(
            n.astype(BF16),
            fw_ref[:, pl.ds(i * PAIR, PAIR)],
            (((1,), (1,)), ((), ())),
            preferred_element_type=F32,
        )

    total_steps = mod_ref.shape[0]
    count = total_steps + 1.0
    step_delta = -1.0 / count
    flow = (total_steps - jnp.full((1, CH), step, jnp.int32).astype(F32)) / count
    sigma = NOISE_LEVEL * jnp.sqrt(flow / (1.0 - flow))
    spread = sigma * math.sqrt(1.0 / count)
    pull = sigma * sigma / (2.0 * flow)

    def drift(state, v):
        return state + (v + pull * (state + (1.0 - flow) * v)) * step_delta

    latent = lat_ref[0]
    noise = noise_ref[0]
    step_mean = drift(latent, velocity)
    mean_ref[0] = step_mean
    shifted = noise + (drift(latent, old_ref[0].astype(F32)) - step_mean) / spread
    gap = noise * noise - shifted * shifted
    gap = jnp.sum(jnp.sum(gap, axis=1, keepdims=True), axis=0, keepdims=True) * 0.5
    rat1[t] = jnp.broadcast_to(gap, (8, 128))
    for j in range(1, 8):
        go(peer_copy(rat1, r1_s, r1_r, "tensor", t, j))
    for j in range(1, 8):
        peer_arrival(rat1, r1_s, r1_r, "tensor", t, j).wait_recv()
    rat2[s] = jnp.sum(rat1[...], axis=0)
    for j in range(1, 8):
        go(peer_copy(rat2, r2_s, r2_r, "seq", s, j))
    for j in range(1, 8):
        peer_arrival(rat2, r2_s, r2_r, "seq", s, j).wait_recv()
    elements = 64 * CH * CH
    ratio = jnp.sum(rat2[...], axis=0) / elements
    ratio_ref[0] = ratio[0, 0]
    for copy in sends:
        copy.wait_send()


def shards(
    image_states,
    text_states,
    image_qkv,
    text_qkv,
    image_out,
    final_weight,
    query_gain,
    key_gain,
    modulation,
    latent,
    old_velocity,
    rollout_noise,
    group_ids,
    text_lengths,
    step_ids,
):
    smem = pl.BlockSpec(memory_space=pltpu.SMEM)
    vmem = pl.BlockSpec(memory_space=pltpu.VMEM)
    hbm = pl.BlockSpec(memory_space=pl.ANY)
    dma = pltpu.SemaphoreType.DMA
    half = WIDTH // 2
    return pl.pallas_call(
        block,
        out_shape=(
            jax.ShapeDtypeStruct(latent.shape, F32),
            jax.ShapeDtypeStruct((1,), F32),
        ),
        in_specs=[smem, smem, smem, vmem, vmem, hbm, hbm, hbm] + [vmem] * 7,
        out_specs=(vmem, smem),
        scratch_shapes=[
            pltpu.VMEM((WIDTH, 3 * FEAT), BF16),
            pltpu.VMEM((WIDTH, 3 * FEAT), BF16),
            pltpu.VMEM((PAIR, WIDTH), BF16),
            pltpu.VMEM((RING, TOK, PAIR), BF16),
            pltpu.VMEM((RING, 8, PAIR), F32),
            pltpu.VMEM((PAD, 128), F32),
            pltpu.VMEM((8, 8, PAD), F32),
            pltpu.VMEM((PAD, 128), F32),
            pltpu.VMEM((TOK, 3 * FEAT), F32),
            pltpu.VMEM((2, IMG, FEAT), BF16),
            pltpu.VMEM((RING, TOK, PAIR), BF16),
            pltpu.VMEM((2, HEADS, VROWS, IMG), F32),
            pltpu.VMEM((RING, FEAT + 16, 128), BF16),
            pltpu.VMEM((RING, FEAT + 16, 128), BF16),
            pltpu.VMEM((RING, 128, FEAT), BF16),
            pltpu.VMEM((RING, CH, PAIR), BF16),
            pltpu.VMEM((2, CH, half), BF16),
            pltpu.VMEM((2, CH, half), BF16),
            pltpu.VMEM((2, CH, half), BF16),
            pltpu.VMEM((CH, WIDTH), F32),
            pltpu.VMEM((2, CH, half), BF16),
            pltpu.VMEM((2, CH, half), BF16),
            pltpu.VMEM((2, CH, half), BF16),
            pltpu.VMEM((8, 8, 128), F32),
            pltpu.VMEM((8, 8, 128), F32),
            dma((7,)),
            dma((8,)),
            dma((8,)),
            dma((2,)),
            dma((2,)),
            dma((2, 2, 3)),
            dma((2, 2, 3)),
            dma((2, 2, 3)),
            dma((2, 2, 3)),
            dma((2, 2, 3)),
            dma((2, 2, 3)),
            dma((2,)),
            dma((2,)),
            dma((RING,)),
            dma((RING,)),
            dma((RING,)),
            dma((RING,)),
            dma((1,)),
            dma((1,)),
            dma((2, 3)),
            dma((2, 3)),
            dma((8,)),
            dma((8,)),
            dma((8,)),
            dma((8,)),
        ],
        compiler_params=pltpu.CompilerParams(
            collective_id=0, has_side_effects=True, vmem_limit_bytes=62 * 1024 * 1024
        ),
    )(
        step_ids,
        group_ids,
        text_lengths,
        image_states,
        text_states,
        jnp.transpose(image_qkv, (1, 0, 2)),
        jnp.transpose(text_qkv, (1, 0, 2)),
        image_out,
        final_weight.T,
        query_gain.reshape(1, HD),
        key_gain.reshape(1, HD),
        modulation,
        latent,
        old_velocity,
        rollout_noise,
    )


def solution(mesh):
    placed = (
        P("dp", "seq", "tensor"),
        P(None, "seq", "tensor"),
        P(None, None, "tensor"),
        P(None, None, "tensor"),
        P("tensor", None),
        P(),
        P(),
        P(),
        P(),
        P("dp", ("seq", "tensor"), None),
        P("dp", ("seq", "tensor"), None),
        P("dp", ("seq", "tensor"), None),
        P("dp"),
        P(),
        P("dp"),
    )
    return jax.shard_map(
        shards,
        mesh=mesh,
        in_specs=placed,
        out_specs=(P("dp", ("seq", "tensor"), None), P("dp")),
        check_vma=False,
    )
```

time: 245 us -> 94.1 us (0.38)
  Pallas kernels: 0 us -> 88.8 us
  waiting for transfers between devices: 72.8 us -> 0 us
  blocking collectives: 48.6 us -> 0 us
  matrix products: 43.5 us -> 0 us
  local copies, waits for them, and re-layouts: 40 us -> 1.38 us
  other arithmetic: 19.9 us -> 0 us
  between operations: 18.8 us -> 3.7 us
    pallas_call x0 -> x1, Pallas kernels: none -> 88.8 us  [shards(): pl.pallas_call(block, out_shape=(jax.ShapeDtypeStruct(latent.shape, F32),...]
    all_gather x3 -> x0, waiting for transfers between devices: 45.6 us -> none  [the longest x1 27.4 us: shards(): lax.all_gather(value_rows, 'seq', axis=1, tiled=True)]
    dot_general x8 -> x0, matrix products: 43.5 us -> none  [the longest x1 14.3 us: shards(): jnp.einsum('sqhd,skhd->shqk', queries, key_piece, preferred_element_type=...]
    unnamed x1 -> x0, blocking collectives: 31.4 us -> none
    reduce_scatter x1 -> x0, waiting for transfers between devices: 27.1 us -> none  [shards(): lax.psum_scatter(jnp.einsum('tsk,kd->tsd', attended, image_out, preferred...]
    unnamed x36 -> x1, local copies, waits for them, and re-layouts: 24.2 us -> 1.38 us
    all_to_all x1 -> x0, blocking collectives: 17.2 us -> none  [from_everyone(): lax.all_to_all(jnp.broadcast_to(value[None], (length, *value.shape)), axi...]
    all_gather x2 -> x0, local copies, waits for them, and re-layouts: 11.6 us -> none  [the longest x1 5.81 us: shards(): lax.all_gather(key_rows, 'seq', axis=1, tiled=True)]
  transfers between devices with their start and end apart: 4 -> 0, of which waited for: 4 -> 0; matrix products, arithmetic and copies ran while one was open for 22% -> 0% of each run, Pallas kernels for 0% -> 0%
where the time goes in v1:
time: 94.1 us; the launch traced here: 93.8 us
  Pallas kernels  88.8 us (94%)
  between operations  3.7 us (4%)
  local copies, waits for them, and re-layouts  1.38 us (1%)
    pallas_call x1, Pallas kernels, shards(): pl.pallas_call(block, out_shape=(jax.ShapeDtypeStruct(latent.shape, F32),...  88.8 us

profile of v1, /device:TPU:1, one launch (start us, length us, event | category | flops | bytes accessed | tf_op | source)
XLA Modules:
  0.0 93.8 jit_solution(10700187536061559558)
XLA Ops:
  1.9 88.8 %shard_map.158 = (f32[1,64,64]{2,1,0:T(8,128)}, f32[1]{0:T(128)}) custom-call(s32[1]{0:T(128)S(6)} %copy.20.step_ref, s32[1]{0:T(128)S(6)} %copy.19.group_ref, s32[4]{0:T(128)} %length_ref.1, bf16[1,512,384]{2,1,0:T(8,128)(2,1)} %x_ref.1, bf16[4,64,384]{2,1,0:T(8,128)(2,1)} %text_ref.1, bf16[3,3072,384]{2,1,0:T(8,128)(2,1)} %bitcast.5, ...), custom_call_target="tpu_custom_call" | custom-call | tf_op jit(solution)/shard_map/pallas_call | solution.py:572
  90.7 1.4 %copy.21 = f32[1,64,64]{2,1,0:T(8,128)} copy(f32[1,64,64]{2,1,0:T(8,128)} %get-tuple-element.4) | data formatting | bytes 32768

commit v2 on v1

--- a/solution.py
+++ b/solution.py
@@ -18,7 +18,7 @@
 HEADS, HD = 3, 128
 CH = 64
 RING = 4
-PARTS = ((0, 256), (256, 320))
+PARTS = ((0, 128), (128, 256), (384, 192))
 VROWS = HD + 16
 PAD = 640
 
@@ -40,14 +40,30 @@
 
 
 def block(
+    step_hbm,
+    group_hbm,
+    length_hbm,
+    x_hbm,
+    text_hbm,
+    wi_hbm,
+    wt_hbm,
+    wo_hbm,
+    fw_hbm,
+    qg_hbm,
+    kg_hbm,
+    mod_hbm,
+    lat_hbm,
+    old_hbm,
+    noise_hbm,
+    mean_ref,
+    ratio_ref,
     step_ref,
     group_ref,
     length_ref,
-    x_ref,
     text_ref,
-    wi_hbm,
-    wt_hbm,
-    wo_hbm,
+    wi,
+    wt,
+    wo,
     fw_ref,
     qg_ref,
     kg_ref,
@@ -55,11 +71,6 @@
     lat_ref,
     old_ref,
     noise_ref,
-    mean_ref,
-    ratio_ref,
-    wi,
-    wt,
-    wo,
     xg,
     modv,
     st_col,
@@ -80,8 +91,7 @@
     ropp,
     rdir,
     racc,
-    rat1,
-    rat2,
+    rat,
     w_sem,
     st_s,
     st_r,
@@ -103,10 +113,8 @@
     wo_r,
     p_s,
     p_r,
-    r1_s,
-    r1_r,
-    r2_s,
-    r2_r,
+    r_s,
+    r_r,
 ):
     t = lax.axis_index("tensor")
     s = lax.axis_index("seq")
@@ -120,20 +128,6 @@
     x_dev = {"seq": (1 - xlo) * RING + z}
     cols = pl.ds(pl.multiple_of(c * FEAT, 128), FEAT)
     mate_cols = pl.ds(pl.multiple_of((1 - c) * FEAT, 128), FEAT)
-
-    loads = []
-    for j in range(3):
-        loads.append(
-            pltpu.make_async_copy(wi_hbm.at[j], wi.at[:, pl.ds(j * FEAT, FEAT)], w_sem.at[j])
-        )
-        loads.append(
-            pltpu.make_async_copy(wt_hbm.at[j], wt.at[:, pl.ds(j * FEAT, FEAT)], w_sem.at[3 + j])
-        )
-    my_wo = wo.at[pl.ds(pl.multiple_of(c * FEAT, 128), FEAT)]
-    wo_load = pltpu.make_async_copy(wo_hbm, my_wo, w_sem.at[6])
-    for copy in loads:
-        copy.start()
-    wo_load.start()
 
     barrier = pltpu.get_barrier_semaphore()
     for j in range(1, 8):
@@ -150,10 +144,90 @@
             device_id_type=pl.DeviceIdType.MESH,
         )
 
+    def local(src, dst, k):
+        copy = pltpu.make_async_copy(src, dst, w_sem.at[k])
+        copy.start()
+        return copy
+
+    x_load = local(x_hbm.at[0], xg.at[y, pl.ds(TXT, IMG), cols], 7)
+    text_load = local(text_hbm, text_ref, 8)
+    group_load = local(group_hbm, group_ref, 9)
+    small = [
+        local(step_hbm, step_ref, 10),
+        local(length_hbm, length_ref, 11),
+        local(mod_hbm, mod_ref, 12),
+        local(qg_hbm, qg_ref, 13),
+        local(kg_hbm, kg_ref, 14),
+    ]
+    loads = []
+    for j in range(3):
+        loads.append(local(wt_hbm.at[j], wt.at[:, pl.ds(j * FEAT, FEAT)], 3 + j))
+        loads.append(local(wi_hbm.at[j], wi.at[:, pl.ds(j * FEAT, FEAT)], j))
+    my_wo = wo.at[pl.ds(pl.multiple_of(c * FEAT, 128), FEAT)]
+    late = [
+        local(wo_hbm, my_wo, 6),
+        local(fw_hbm, fw_ref, 15),
+        local(lat_hbm.at[0], lat_ref, 16),
+        local(old_hbm.at[0], old_ref, 17),
+        local(noise_hbm.at[0], noise_ref, 18),
+    ]
+
+    text_load.wait()
+    group_load.wait()
     group = group_ref[0]
-    step = step_ref[0]
     xg[y, pl.ds(0, TXT), cols] = text_ref[group]
-    xg[y, pl.ds(TXT, IMG), cols] = x_ref[0]
+    x_load.wait()
+    pl.semaphore_wait(barrier, 14)
+
+    def peer_copy(buf, send, recv, axis, me, j):
+        slot = buf.at[me]
+        return remote(slot, slot, send.at[j], recv.at[j], {axis: lax.rem(me + j, 8)})
+
+    def peer_arrival(buf, send, recv, axis, me, j):
+        slot = buf.at[lax.rem(me + 8 - j, 8)]
+        return remote(slot, slot, send.at[j], recv.at[j], {axis: lax.rem(me + j, 8)})
+
+    def y_slot(d, k, sending):
+        if k < 2:
+            return (y if sending else (ym, yp)[d]), (k if d == 0 else 1 - k)
+        return ((ym, yp)[d] if sending else yo), d
+
+    def y_send(d, part, k):
+        slot, sub = y_slot(d, k, True)
+        ref = xg.at[slot, piece(part, sub), cols]
+        return remote(ref, ref, y_s.at[d, part, k], y_r.at[d, part, k], y_dev[d])
+
+    def y_arrival(d, part, k):
+        slot, sub = y_slot(d, k, False)
+        ref = xg.at[slot, piece(part, sub), cols]
+        return remote(ref, ref, y_s.at[d, part, k], y_r.at[d, part, k], y_dev[d])
+
+    def relay(d, part, k):
+        slot, sub = y_slot(d, k, False)
+        ref = xg.at[slot, piece(part, sub), cols]
+        return remote(ref, ref, l_s.at[d, part, k], l_r.at[d, part, k], mate)
+
+    def relay_arrival(d, part, k):
+        slot, sub = y_slot(d, k, False)
+        ref = xg.at[slot, piece(part, sub), mate_cols]
+        return remote(ref, ref, l_s.at[d, part, k], l_r.at[d, part, k], mate)
+
+    def own_copy(columns):
+        ref = xg.at[y, :, columns]
+        return remote(ref, ref, own_s.at[0], own_r.at[0], mate)
+
+    sends = []
+
+    def go(copy):
+        copy.start()
+        sends.append(copy)
+
+    def y_own(part):
+        for k in range(2):
+            for d in range(2):
+                go(y_send(d, part, k))
+
+    y_own(0)
 
     mine = xg[y, :, cols].astype(F32)
     part_mean = jnp.mean(mine, axis=-1, keepdims=True)
@@ -162,68 +236,35 @@
     lane = lax.broadcasted_iota(jnp.int32, (TOK, 128), 1)
     st_col[pl.ds(0, TOK), :] = jnp.where(lane == 0, part_mean, jnp.where(lane == 1, part_sq, 0.0))
     st_col[pl.ds(TOK, PAD - TOK), :] = jnp.zeros((PAD - TOK, 128), F32)
-    st_all[t] = st_col[...].T[0:8, :]
-
+    st_all[t] = st_col[...].T[0:2, :]
+    for j in range(1, 8):
+        go(peer_copy(st_all, st_s, st_r, "tensor", t, j))
+    go(own_copy(cols))
+
+    def y_first(part):
+        for d in range(2):
+            y_arrival(d, part, 0).wait_recv()
+            go(y_send(d, part, 2))
+            go(relay(d, part, 0))
+
+    def y_relay(part, k):
+        for d in range(2):
+            y_arrival(d, part, k).wait_recv()
+            go(relay(d, part, k))
+
+    def y_ready(part, k):
+        for d in range(2):
+            relay_arrival(d, part, k).wait_recv()
+
+    for copy in small:
+        copy.wait()
+    step = step_ref[0]
     for i in range(RING):
         modv[i, pl.ds(0, 7), :] = mod_ref[step, :, pl.ds(i * PAIR, PAIR)]
 
-    pl.semaphore_wait(barrier, 14)
-
-    def peer_copy(buf, send, recv, axis, me, j):
-        slot = buf.at[me]
-        return remote(slot, slot, send.at[j], recv.at[j], {axis: lax.rem(me + j, 8)})
-
-    def peer_arrival(buf, send, recv, axis, me, j):
-        slot = buf.at[lax.rem(me + 8 - j, 8)]
-        return remote(slot, slot, send.at[j], recv.at[j], {axis: lax.rem(me + j, 8)})
-
-    stat_sends = [peer_copy(st_all, st_s, st_r, "tensor", t, j) for j in range(1, 8)]
-    for copy in stat_sends:
-        copy.start()
-
-    def y_slot(d, k, sending):
-        if k < 2:
-            return (y if sending else (ym, yp)[d]), (k if d == 0 else 1 - k)
-        return ((ym, yp)[d] if sending else yo), d
-
-    def y_send(d, part, k):
-        slot, sub = y_slot(d, k, True)
-        ref = xg.at[slot, piece(part, sub), cols]
-        return remote(ref, ref, y_s.at[d, part, k], y_r.at[d, part, k], y_dev[d])
-
-    def y_arrival(d, part, k):
-        slot, sub = y_slot(d, k, False)
-        ref = xg.at[slot, piece(part, sub), cols]
-        return remote(ref, ref, y_s.at[d, part, k], y_r.at[d, part, k], y_dev[d])
-
-    def relay(d, part, k):
-        slot, sub = y_slot(d, k, False)
-        ref = xg.at[slot, piece(part, sub), cols]
-        return remote(ref, ref, l_s.at[d, part, k], l_r.at[d, part, k], mate)
-
-    def relay_arrival(d, part, k):
-        slot, sub = y_slot(d, k, False)
-        ref = xg.at[slot, piece(part, sub), mate_cols]
-        return remote(ref, ref, l_s.at[d, part, k], l_r.at[d, part, k], mate)
-
-    def own_copy(part, columns):
-        ref = xg.at[y, pl.ds(*PARTS[part]), columns]
-        return remote(ref, ref, own_s.at[part], own_r.at[part], mate)
-
-    sends = list(stat_sends)
-
-    def go(copy):
-        copy.start()
-        sends.append(copy)
-
-    def y_own(part):
-        for k in range(2):
-            for d in range(2):
-                go(y_send(d, part, k))
-
-    y_own(0)
-    go(own_copy(0, cols))
-    go(own_copy(1, cols))
+    y_first(0)
+    y_own(1)
+    y_relay(0, 1)
 
     for j in range(1, 8):
         peer_arrival(st_all, st_s, st_r, "tensor", t, j).wait_recv()
@@ -308,93 +349,113 @@
             for d in range(2):
                 go(z_send(d, part, k))
 
-    for part in range(2):
-        own_copy(part, mate_cols).wait_recv()
-        project(y, part, first=True)
+    def z_first(part):
         for d in range(2):
-            y_arrival(d, part, 0).wait_recv()
-            go(y_send(d, part, 2))
-            go(relay(d, part, 0))
-        if part == 0:
-            y_own(1)
+            z_arrival(d, part, 0).wait_recv()
+            go(z_send(d, part, 2))
+
+    def z_wait(part, k):
         for d in range(2):
-            y_arrival(d, part, 1).wait_recv()
-            go(relay(d, part, 1))
-        for k in range(2):
-            for d in range(2):
-                relay_arrival(d, part, k).wait_recv()
-        project(ym, part)
-        project(yp, part)
-        for d in range(2):
-            y_arrival(d, part, 2).wait_recv()
-            go(relay(d, part, 2))
-        for d in range(2):
-            relay_arrival(d, part, 2).wait_recv()
-        project(yo, part)
-        finish(part)
-        if part == 0:
-            z_own(0)
-        go(q_copy(part))
-
-    wo_load.wait()
+            z_arrival(d, part, k).wait_recv()
+
+    own_copy(mate_cols).wait_recv()
+    project(y, 0, first=True)
+    y_ready(0, 0)
+    y_ready(0, 1)
+    project(ym, 0)
+    project(yp, 0)
+    y_relay(0, 2)
+    y_ready(0, 2)
+    project(yo, 0)
+    finish(0)
+    z_own(0)
+    go(q_copy(0))
+
+    y_first(1)
+    y_own(2)
+    project(y, 1, first=True)
+    y_relay(1, 1)
+    y_ready(1, 0)
+    y_ready(1, 1)
+    project(ym, 1)
+    project(yp, 1)
+    z_first(0)
+    y_relay(1, 2)
+    project(y, 2, first=True)
+    y_ready(1, 2)
+    project(yo, 1)
+    finish(1)
+    z_own(1)
+    go(q_copy(1))
+
+    y_first(2)
+    y_relay(2, 1)
+    y_ready(2, 0)
+    y_ready(2, 1)
+    project(ym, 2)
+    project(yp, 2)
+    y_relay(2, 2)
+    y_ready(2, 2)
+    project(yo, 2)
+    finish(2)
+    go(q_copy(2))
+
+    for copy in late:
+        copy.wait()
     wo_send = remote(my_wo, my_wo, wo_s.at[0], wo_r.at[0], mate)
     go(wo_send)
 
     length = length_ref[group]
 
-    def attend(slot, part, sets, first=False):
-        start, rows = PARTS[part]
-        at = pl.ds(start, rows)
-
-        def one_head(h, carry):
-            at_k = pl.ds(pl.multiple_of(h * HD, 128), HD)
-            at_v = pl.ds(pl.multiple_of(FEAT + h * HD, 128), HD)
-            keys = kv[slot, at, at_k]
-            vals = kv[slot, at, at_v].astype(F32).T
-            ones = jnp.ones((VROWS - HD, rows), F32)
-            if part == 0:
-                pos = lax.broadcasted_iota(jnp.int32, (1, rows), 1)
-                used = (pos >= TXT) | (pos + (xlo * RING + slot) * TXT < length)
-                vals = jnp.where(used, vals, 0.0)
-                ones = jnp.where(used, ones, 0.0)
-            ext = jnp.concatenate([vals, ones], axis=0).astype(BF16)
+    def values(slot, start, rows, h):
+        vals = kv[slot, pl.ds(start, rows), pl.ds(FEAT + h * HD, HD)].astype(F32).T
+        ones = jnp.ones((VROWS - HD, rows), F32)
+        if start == 0:
+            pos = lax.broadcasted_iota(jnp.int32, (1, rows), 1)
+            used = (pos >= TXT) | (pos + (xlo * RING + slot) * TXT < length)
+            vals = jnp.where(used, vals, 0.0)
+            ones = jnp.where(used, ones, 0.0)
+        return jnp.concatenate([vals, ones], axis=0).astype(BF16)
+
+    def weighted(slot, start, rows, h, ext, q, at_q):
+        scores = lax.dot_general(
+            kv[slot, pl.ds(start, rows), pl.ds(h * HD, HD)],
+            qall[q, at_q, pl.ds(h * HD, HD)],
+            (((1,), (1,)), ((), ())),
+            preferred_element_type=F32,
+        )
+        return jnp.dot(ext, jnp.exp2(scores).astype(BF16), preferred_element_type=F32)
+
+    def attend(slot, start, rows, sets, first=False):
+        for h in range(HEADS):
+            ext = values(slot, start, rows, h)
             for q in sets:
-                scores = lax.dot_general(
-                    keys,
-                    qall[q, :, at_k],
-                    (((1,), (1,)), ((), ())),
-                    preferred_element_type=F32,
-                )
-                e = jnp.exp2(scores).astype(BF16)
-                o = jnp.dot(ext, e, preferred_element_type=F32)
+                o = weighted(slot, start, rows, h, ext, q, pl.ds(0, IMG))
                 if first:
                     oacc[q, h] = o
                 else:
                     oacc[q, h] += o
-            return carry
-
-        lax.fori_loop(0, HEADS, one_head, 0)
-
-    for part in range(2):
-        for d in range(2):
-            z_arrival(d, part, 0).wait_recv()
-            go(z_send(d, part, 2))
-        if part == 0:
-            z_own(1)
-            q_wait = [q_copy(0), q_copy(1)]
-            for copy in q_wait:
-                copy.wait_recv()
-            attend(z, 0, (1, 0), first=True)
-            attend(z, 1, (1, 0))
-        for d in range(2):
-            z_arrival(d, part, 1).wait_recv()
-        attend(zm, part, (1, 0))
-        attend(zp, part, (1, 0))
-        for d in range(2):
-            z_arrival(d, part, 2).wait_recv()
-        if part == 0:
-            attend(zo, part, (1, 0))
-    attend(zo, 1, (1,))
+
+    attend(z, 0, TOK, (0,), first=True)
+    z_first(1)
+    z_own(2)
+    z_wait(0, 1)
+    z_wait(0, 2)
+    for part in range(3):
+        q_copy(part).wait_recv()
+    attend(z, 0, TOK, (1,), first=True)
+    for slot in (zm, zp, zo):
+        attend(slot, *PARTS[0], (1, 0))
+    z_wait(1, 1)
+    attend(zm, *PARTS[1], (1, 0))
+    attend(zp, *PARTS[1], (1, 0))
+    z_first(2)
+    z_wait(1, 2)
+    attend(zo, *PARTS[1], (1, 0))
+    z_wait(2, 1)
+    attend(zm, *PARTS[2], (1, 0))
+    attend(zp, *PARTS[2], (1, 0))
+    z_wait(2, 2)
 
     order = (yo, yp, ym, y)
 
@@ -404,11 +465,15 @@
     def lanes(i):
         return pl.ds(pl.multiple_of(i * 128, 128), 128)
 
+    last = [values(zo, *PARTS[2], h) for h in range(HEADS)]
     for j in range(RING):
         at = lanes(order[j])
+        dens = []
         for h in range(HEADS):
-            osend[j, pl.ds(h * HD, HD), :] = oacc[1, h, pl.ds(0, HD), at].astype(BF16)
-        whole = jnp.concatenate([oacc[1, h, pl.ds(HD, 1), at] for h in range(HEADS)], axis=0)
+            o = oacc[1, h, :, at] + weighted(zo, *PARTS[2], h, last[h], 1, at)
+            osend[j, pl.ds(h * HD, HD), :] = o[:HD].astype(BF16)
+            dens.append(o[HD : HD + 1])
+        whole = jnp.concatenate(dens, axis=0)
         high = whole.astype(BF16)
         rest = whole - high.astype(F32)
         middle = rest.astype(BF16)
@@ -418,7 +483,7 @@
             axis=0,
         ).astype(BF16)
         go(o_copy(j))
-    attend(zo, 1, (0,))
+    attend(zo, *PARTS[2], (0,))
 
     def a_copy(j, columns):
         return remote(
@@ -452,37 +517,35 @@
         dst = (ropp.at[d], rdir.at[d], racc.at[d])[k]
         return remote(src, dst, p_s.at[d, k], p_r.at[d, k], y_dev[d])
 
-    def out_rows(j):
+    def out_side(j, d):
+        return jnp.dot(attb[j], wo[:, sides[d]], preferred_element_type=F32)
+
+    def dispatch(j):
         a_copy(j, mate_cols).wait_recv()
-        return jnp.dot(attb[j], wo[...], preferred_element_type=F32)
-
-    def dispatch(j):
-        p = out_rows(j)
         if j == 0:
             for d in range(2):
-                pso[d] = p[:, d * half : (d + 1) * half].astype(BF16)
+                pso[d] = out_side(0, d).astype(BF16)
                 go(p_copy(d, 0))
-        elif j < 3:
-            d = j - 1
-            keep, direct = d, 1 - d
-            pdir[d] = p[:, direct * half : (direct + 1) * half].astype(BF16)
-            go(p_copy(d, 1))
-            pown[:, sides[keep]] = p[:, keep * half : (keep + 1) * half]
+        else:
+            keep, direct = j - 1, 2 - j
+            pdir[keep] = out_side(j, direct).astype(BF16)
+            go(p_copy(keep, 1))
+            pown[:, sides[keep]] = out_side(j, keep)
 
     remote(my_wo, wo.at[pl.ds(pl.multiple_of((1 - c) * FEAT, 128), FEAT)], wo_s.at[0], wo_r.at[0], mate).wait_recv()
     for j in range(RING):
         combine(j)
         if j >= 1:
             dispatch(j - 1)
-    last = out_rows(3)
+    a_copy(3, mate_cols).wait_recv()
+    mine = [out_side(3, d) for d in range(2)]
     for d in range(2):
         p_copy(d, 0).wait_recv()
         pacc[d] = (pown[:, sides[d]] + ropp[d].astype(F32)).astype(BF16)
         go(p_copy(d, 2))
-    pown[...] = last
     for d in range(2):
-        p_copy(d, 1).wait_recv()
-        pown[:, sides[1 - d]] += rdir[d].astype(F32)
+        p_copy(1 - d, 1).wait_recv()
+        pown[:, sides[d]] = mine[d] + rdir[1 - d].astype(F32)
     for d in range(2):
         p_copy(d, 2).wait_recv()
         pown[:, sides[d]] += racc[d].astype(F32)
@@ -523,26 +586,30 @@
     def drift(state, v):
         return state + (v + pull * (state + (1.0 - flow) * v)) * step_delta
 
-    latent = lat_ref[0]
-    noise = noise_ref[0]
+    latent = lat_ref[...]
+    noise = noise_ref[...]
     step_mean = drift(latent, velocity)
     mean_ref[0] = step_mean
-    shifted = noise + (drift(latent, old_ref[0].astype(F32)) - step_mean) / spread
+    shifted = noise + (drift(latent, old_ref[...].astype(F32)) - step_mean) / spread
     gap = noise * noise - shifted * shifted
     gap = jnp.sum(jnp.sum(gap, axis=1, keepdims=True), axis=0, keepdims=True) * 0.5
-    rat1[t] = jnp.broadcast_to(gap, (8, 128))
-    for j in range(1, 8):
-        go(peer_copy(rat1, r1_s, r1_r, "tensor", t, j))
-    for j in range(1, 8):
-        peer_arrival(rat1, r1_s, r1_r, "tensor", t, j).wait_recv()
-    rat2[s] = jnp.sum(rat1[...], axis=0)
-    for j in range(1, 8):
-        go(peer_copy(rat2, r2_s, r2_r, "seq", s, j))
-    for j in range(1, 8):
-        peer_arrival(rat2, r2_s, r2_r, "seq", s, j).wait_recv()
+    me = s * 8 + t
+    rat[me] = jnp.broadcast_to(gap, (1, 128))
+
+    def tell(j, carry):
+        other = lax.rem(me + j, 64)
+        where = {"seq": lax.div(other, 8), "tensor": lax.rem(other, 8)}
+        remote(rat.at[me], rat.at[me], r_s.at[0], r_r.at[0], where).start()
+        return carry
+
+    lax.fori_loop(1, 64, tell, 0)
+    told = rat.at[pl.ds(0, 63)]
+    everyone = remote(told, told, r_s.at[0], r_r.at[0], mate)
+    everyone.wait_recv()
     elements = 64 * CH * CH
-    ratio = jnp.sum(rat2[...], axis=0) / elements
+    ratio = jnp.sum(rat[...], axis=0) / elements
     ratio_ref[0] = ratio[0, 0]
+    everyone.wait_send()
     for copy in sends:
         copy.wait_send()
 
@@ -575,16 +642,27 @@
             jax.ShapeDtypeStruct(latent.shape, F32),
             jax.ShapeDtypeStruct((1,), F32),
         ),
-        in_specs=[smem, smem, smem, vmem, vmem, hbm, hbm, hbm] + [vmem] * 7,
+        in_specs=[hbm] * 15,
         out_specs=(vmem, smem),
         scratch_shapes=[
+            pltpu.SMEM((1,), jnp.int32),
+            pltpu.SMEM((1,), jnp.int32),
+            pltpu.SMEM((4,), jnp.int32),
+            pltpu.VMEM(text_states.shape, BF16),
             pltpu.VMEM((WIDTH, 3 * FEAT), BF16),
             pltpu.VMEM((WIDTH, 3 * FEAT), BF16),
             pltpu.VMEM((PAIR, WIDTH), BF16),
+            pltpu.VMEM((CH, WIDTH), BF16),
+            pltpu.VMEM((1, HD), F32),
+            pltpu.VMEM((1, HD), F32),
+            pltpu.VMEM(modulation.shape, F32),
+            pltpu.VMEM((CH, CH), F32),
+            pltpu.VMEM((CH, CH), BF16),
+            pltpu.VMEM((CH, CH), F32),
             pltpu.VMEM((RING, TOK, PAIR), BF16),
             pltpu.VMEM((RING, 8, PAIR), F32),
             pltpu.VMEM((PAD, 128), F32),
-            pltpu.VMEM((8, 8, PAD), F32),
+            pltpu.VMEM((8, 2, PAD), F32),
             pltpu.VMEM((PAD, 128), F32),
             pltpu.VMEM((TOK, 3 * FEAT), F32),
             pltpu.VMEM((2, IMG, FEAT), BF16),
@@ -601,21 +679,20 @@
             pltpu.VMEM((2, CH, half), BF16),
             pltpu.VMEM((2, CH, half), BF16),
             pltpu.VMEM((2, CH, half), BF16),
-            pltpu.VMEM((8, 8, 128), F32),
-            pltpu.VMEM((8, 8, 128), F32),
-            dma((7,)),
+            pltpu.VMEM((64, 1, 128), F32),
+            dma((19,)),
             dma((8,)),
             dma((8,)),
-            dma((2,)),
-            dma((2,)),
-            dma((2, 2, 3)),
-            dma((2, 2, 3)),
-            dma((2, 2, 3)),
-            dma((2, 2, 3)),
-            dma((2, 2, 3)),
-            dma((2, 2, 3)),
-            dma((2,)),
-            dma((2,)),
+            dma((1,)),
+            dma((1,)),
+            dma((2, 3, 3)),
+            dma((2, 3, 3)),
+            dma((2, 3, 3)),
+            dma((2, 3, 3)),
+            dma((2, 3, 3)),
+            dma((2, 3, 3)),
+            dma((3,)),
+            dma((3,)),
             dma((RING,)),
             dma((RING,)),
             dma((RING,)),
@@ -624,10 +701,8 @@
             dma((1,)),
             dma((2, 3)),
             dma((2, 3)),
-            dma((8,)),
-            dma((8,)),
-            dma((8,)),
-            dma((8,)),
+            dma((1,)),
+            dma((1,)),
         ],
         compiler_params=pltpu.CompilerParams(
             collective_id=0, has_side_effects=True, vmem_limit_bytes=62 * 1024 * 1024

time: 94.1 us -> 84.9 us (0.902)
  Pallas kernels: 88.8 us -> 79.6 us
    pallas_call x1, Pallas kernels: 88.8 us -> 79.6 us  [shards(): pl.pallas_call(block, out_shape=(jax.ShapeDtypeStruct(latent.shape, F32),...]
where the time goes in v2:
time: 84.9 us; the launch traced here: 84.7 us
  Pallas kernels  79.6 us (94%)
  between operations  3.7 us (4%)
  local copies, waits for them, and re-layouts  1.38 us (2%)
    pallas_call x1, Pallas kernels, shards(): pl.pallas_call(block, out_shape=(jax.ShapeDtypeStruct(latent.shape, F32),...  79.6 us

profile of v2, /device:TPU:1, one launch (start us, length us, event | category | flops | bytes accessed | tf_op | source)
XLA Modules:
  0.0 84.7 jit_solution(8390730113128058710)
XLA Ops:
  1.9 79.6 %shard_map.158 = (f32[1,64,64]{2,1,0:T(8,128)}, f32[1]{0:T(128)}) custom-call(s32[1]{0:T(128)S(6)} %copy.20.step_hbm, s32[1]{0:T(128)S(6)} %copy.19.group_hbm, s32[4]{0:T(128)} %length_hbm.1, bf16[1,512,384]{2,1,0:T(8,128)(2,1)} %x_hbm.1, bf16[4,64,384]{2,1,0:T(8,128)(2,1)} %text_hbm.1, bf16[3,3072,384]{2,1,0:T(8,128)(2,1)} %bitcast.5, ...), custom_call_target="tpu_custom_call" | custom-call | tf_op jit(solution)/shard_map/pallas_call | solution.py:639
  81.6 1.4 %copy.21 = f32[1,64,64]{2,1,0:T(8,128)} copy(f32[1,64,64]{2,1,0:T(8,128)} %get-tuple-element.4) | data formatting | bytes 32768

commit v3 on v2

--- a/solution.py
+++ b/solution.py
@@ -18,7 +18,9 @@
 HEADS, HD = 3, 128
 CH = 64
 RING = 4
+HEAD_ROWS = 128
 PARTS = ((0, 128), (128, 256), (384, 192))
+GROUPS = ((0, 0, 3),) + tuple((part, h, 1) for h in range(3) for part in (1, 2))
 VROWS = HD + 16
 PAD = 640
 
@@ -149,7 +151,11 @@
         copy.start()
         return copy
 
-    x_load = local(x_hbm.at[0], xg.at[y, pl.ds(TXT, IMG), cols], 7)
+    head_rows = pl.ds(0, HEAD_ROWS)
+    rest_rows = pl.ds(HEAD_ROWS, IMG - HEAD_ROWS)
+    moved_rows = pl.ds(HEAD_ROWS + TXT, IMG - HEAD_ROWS)
+    x_load = local(x_hbm.at[0, head_rows], xg.at[y, head_rows, cols], 7)
+    x_rest = local(x_hbm.at[0, rest_rows], xg.at[y, moved_rows, cols], 19)
     text_load = local(text_hbm, text_ref, 8)
     group_load = local(group_hbm, group_ref, 9)
     small = [
@@ -175,59 +181,9 @@
     text_load.wait()
     group_load.wait()
     group = group_ref[0]
-    xg[y, pl.ds(0, TXT), cols] = text_ref[group]
+    xg[y, pl.ds(HEAD_ROWS, TXT), cols] = text_ref[group]
     x_load.wait()
-    pl.semaphore_wait(barrier, 14)
-
-    def peer_copy(buf, send, recv, axis, me, j):
-        slot = buf.at[me]
-        return remote(slot, slot, send.at[j], recv.at[j], {axis: lax.rem(me + j, 8)})
-
-    def peer_arrival(buf, send, recv, axis, me, j):
-        slot = buf.at[lax.rem(me + 8 - j, 8)]
-        return remote(slot, slot, send.at[j], recv.at[j], {axis: lax.rem(me + j, 8)})
-
-    def y_slot(d, k, sending):
-        if k < 2:
-            return (y if sending else (ym, yp)[d]), (k if d == 0 else 1 - k)
-        return ((ym, yp)[d] if sending else yo), d
-
-    def y_send(d, part, k):
-        slot, sub = y_slot(d, k, True)
-        ref = xg.at[slot, piece(part, sub), cols]
-        return remote(ref, ref, y_s.at[d, part, k], y_r.at[d, part, k], y_dev[d])
-
-    def y_arrival(d, part, k):
-        slot, sub = y_slot(d, k, False)
-        ref = xg.at[slot, piece(part, sub), cols]
-        return remote(ref, ref, y_s.at[d, part, k], y_r.at[d, part, k], y_dev[d])
-
-    def relay(d, part, k):
-        slot, sub = y_slot(d, k, False)
-        ref = xg.at[slot, piece(part, sub), cols]
-        return remote(ref, ref, l_s.at[d, part, k], l_r.at[d, part, k], mate)
-
-    def relay_arrival(d, part, k):
-        slot, sub = y_slot(d, k, False)
-        ref = xg.at[slot, piece(part, sub), mate_cols]
-        return remote(ref, ref, l_s.at[d, part, k], l_r.at[d, part, k], mate)
-
-    def own_copy(columns):
-        ref = xg.at[y, :, columns]
-        return remote(ref, ref, own_s.at[0], own_r.at[0], mate)
-
-    sends = []
-
-    def go(copy):
-        copy.start()
-        sends.append(copy)
-
-    def y_own(part):
-        for k in range(2):
-            for d in range(2):
-                go(y_send(d, part, k))
-
-    y_own(0)
+    x_rest.wait()
 
     mine = xg[y, :, cols].astype(F32)
     part_mean = jnp.mean(mine, axis=-1, keepdims=True)
@@ -237,8 +193,60 @@
     st_col[pl.ds(0, TOK), :] = jnp.where(lane == 0, part_mean, jnp.where(lane == 1, part_sq, 0.0))
     st_col[pl.ds(TOK, PAD - TOK), :] = jnp.zeros((PAD - TOK, 128), F32)
     st_all[t] = st_col[...].T[0:2, :]
+
+    pl.semaphore_wait(barrier, 14)
+
+    def peer_copy(buf, send, recv, axis, me, j):
+        slot = buf.at[me]
+        return remote(slot, slot, send.at[j], recv.at[j], {axis: lax.rem(me + j, 8)})
+
+    def peer_arrival(buf, send, recv, axis, me, j):
+        slot = buf.at[lax.rem(me + 8 - j, 8)]
+        return remote(slot, slot, send.at[j], recv.at[j], {axis: lax.rem(me + j, 8)})
+
+    def y_slot(d, k, sending):
+        if k < 2:
+            return (y if sending else (ym, yp)[d]), (k if d == 0 else 1 - k)
+        return ((ym, yp)[d] if sending else yo), d
+
+    def y_send(d, part, k):
+        slot, sub = y_slot(d, k, True)
+        ref = xg.at[slot, piece(part, sub), cols]
+        return remote(ref, ref, y_s.at[d, part, k], y_r.at[d, part, k], y_dev[d])
+
+    def y_arrival(d, part, k):
+        slot, sub = y_slot(d, k, False)
+        ref = xg.at[slot, piece(part, sub), cols]
+        return remote(ref, ref, y_s.at[d, part, k], y_r.at[d, part, k], y_dev[d])
+
+    def relay(d, part, k):
+        slot, sub = y_slot(d, k, False)
+        ref = xg.at[slot, piece(part, sub), cols]
+        return remote(ref, ref, l_s.at[d, part, k], l_r.at[d, part, k], mate)
+
+    def relay_arrival(d, part, k):
+        slot, sub = y_slot(d, k, False)
+        ref = xg.at[slot, piece(part, sub), mate_cols]
+        return remote(ref, ref, l_s.at[d, part, k], l_r.at[d, part, k], mate)
+
+    def own_copy(columns):
+        ref = xg.at[y, :, columns]
+        return remote(ref, ref, own_s.at[0], own_r.at[0], mate)
+
+    sends = []
+
+    def go(copy):
+        copy.start()
+        sends.append(copy)
+
+    def y_own(part):
+        for k in range(2):
+            for d in range(2):
+                go(y_send(d, part, k))
+
     for j in range(1, 8):
         go(peer_copy(st_all, st_s, st_r, "tensor", t, j))
+    y_own(0)
     go(own_copy(cols))
 
     def y_first(part):
@@ -296,9 +304,9 @@
 
     def project(slot, part, first=False):
         start, rows = PARTS[part]
-        if part == 0:
-            project_rows(slot, TXT, rows - TXT, wi, 0, 1, first)
-            project_rows(slot, 0, TXT, wt, 3, 4, first)
+        if part == 1:
+            project_rows(slot, start + TXT, rows - TXT, wi, 0, 1, first)
+            project_rows(slot, start, TXT, wt, 3, 4, first)
         else:
             project_rows(slot, start, rows, wi, 0, 1, first)
 
@@ -308,19 +316,25 @@
         square = jnp.mean(values * values, axis=-1, keepdims=True)
         return (values * lax.rsqrt(square + NORM_EPSILON) * gain).astype(BF16)
 
+    def q_rows(part):
+        start, rows = PARTS[part]
+        if part == 0:
+            return start, start, rows
+        skip = TXT if part == 1 else 0
+        return start + skip, start + skip - TXT, rows - skip
+
     def finish(part):
-        start, rows = PARTS[part]
-        at = pl.ds(start, rows)
+        at = pl.ds(*PARTS[part])
         for h in range(HEADS):
             keys = acc[at, pl.ds(FEAT + h * HD, HD)]
-            kv[z, at, pl.ds(h * HD, HD)] = head_norm(keys, kg_ref[...])
-        kv[z, at, pl.ds(FEAT, FEAT)] = acc[at, pl.ds(2 * FEAT, FEAT)].astype(BF16)
-        first = max(start, TXT)
-        img = pl.ds(first, start + rows - first)
+            kv[z, at, pl.ds(2 * h * HD, HD)] = head_norm(keys, kg_ref[...])
+            vals = acc[at, pl.ds(2 * FEAT + h * HD, HD)]
+            kv[z, at, pl.ds((2 * h + 1) * HD, HD)] = vals.astype(BF16)
+        token, query, rows = q_rows(part)
         for h in range(HEADS):
-            query = acc[img, pl.ds(h * HD, HD)]
-            qall[0, pl.ds(first - TXT, start + rows - first), pl.ds(h * HD, HD)] = head_norm(
-                query, qg_ref[...] * score_scale
+            q = acc[pl.ds(token, rows), pl.ds(h * HD, HD)]
+            qall[0, pl.ds(query, rows), pl.ds(h * HD, HD)] = head_norm(
+                q, qg_ref[...] * score_scale
             )
 
     def z_slot(d, k, sending):
@@ -328,35 +342,30 @@
             return (z if sending else (zm, zp)[d]), (k if d == 0 else 1 - k)
         return ((zm, zp)[d] if sending else zo), d
 
-    def z_send(d, part, k):
-        slot, sub = z_slot(d, k, True)
-        ref = kv.at[slot, piece(part, sub)]
-        return remote(ref, ref, z_s.at[d, part, k], z_r.at[d, part, k], z_dev[d])
-
-    def z_arrival(d, part, k):
-        slot, sub = z_slot(d, k, False)
-        ref = kv.at[slot, piece(part, sub)]
-        return remote(ref, ref, z_s.at[d, part, k], z_r.at[d, part, k], z_dev[d])
+    def z_copy(d, g, k, sending):
+        slot, sub = z_slot(d, k, sending)
+        part, h, heads = GROUPS[g]
+        ref = kv.at[slot, piece(part, sub), pl.ds(2 * h * HD, 2 * heads * HD)]
+        return remote(ref, ref, z_s.at[d, g, k], z_r.at[d, g, k], z_dev[d])
 
     def q_copy(part):
-        start, rows = PARTS[part]
-        first = max(start, TXT)
-        at = pl.ds(first - TXT, start + rows - first)
+        _, query, rows = q_rows(part)
+        at = pl.ds(query, rows)
         return remote(qall.at[0, at], qall.at[1, at], q_s.at[part], q_r.at[part], x_dev)
 
-    def z_own(part):
+    def z_own(g):
         for k in range(2):
             for d in range(2):
-                go(z_send(d, part, k))
-
-    def z_first(part):
+                go(z_copy(d, g, k, True))
+
+    def z_first(g):
         for d in range(2):
-            z_arrival(d, part, 0).wait_recv()
-            go(z_send(d, part, 2))
-
-    def z_wait(part, k):
+            z_copy(d, g, 0, False).wait_recv()
+            go(z_copy(d, g, 2, True))
+
+    def z_wait(g, k):
         for d in range(2):
-            z_arrival(d, part, k).wait_recv()
+            z_copy(d, g, k, False).wait_recv()
 
     own_copy(mate_cols).wait_recv()
     project(y, 0, first=True)
@@ -386,6 +395,7 @@
     project(yo, 1)
     finish(1)
     z_own(1)
+    z_own(3)
     go(q_copy(1))
 
     y_first(2)
@@ -394,10 +404,12 @@
     y_ready(2, 1)
     project(ym, 2)
     project(yp, 2)
+    z_first(1)
     y_relay(2, 2)
     y_ready(2, 2)
     project(yo, 2)
     finish(2)
+    z_own(2)
     go(q_copy(2))
 
     for copy in late:
@@ -408,82 +420,107 @@
     length = length_ref[group]
 
     def values(slot, start, rows, h):
-        vals = kv[slot, pl.ds(start, rows), pl.ds(FEAT + h * HD, HD)].astype(F32).T
+        at = pl.ds(start, rows)
+        vals = kv[slot, at, pl.ds((2 * h + 1) * HD, HD)].astype(F32).T
         ones = jnp.ones((VROWS - HD, rows), F32)
-        if start == 0:
-            pos = lax.broadcasted_iota(jnp.int32, (1, rows), 1)
-            used = (pos >= TXT) | (pos + (xlo * RING + slot) * TXT < length)
+        if start <= HEAD_ROWS:
+            pos = start - HEAD_ROWS + lax.broadcasted_iota(jnp.int32, (1, rows), 1)
+            used = (pos < 0) | (pos >= TXT) | (pos + (xlo * RING + slot) * TXT < length)
             vals = jnp.where(used, vals, 0.0)
             ones = jnp.where(used, ones, 0.0)
         return jnp.concatenate([vals, ones], axis=0).astype(BF16)
 
     def weighted(slot, start, rows, h, ext, q, at_q):
         scores = lax.dot_general(
-            kv[slot, pl.ds(start, rows), pl.ds(h * HD, HD)],
+            kv[slot, pl.ds(start, rows), pl.ds(2 * h * HD, HD)],
             qall[q, at_q, pl.ds(h * HD, HD)],
             (((1,), (1,)), ((), ())),
             preferred_element_type=F32,
         )
         return jnp.dot(ext, jnp.exp2(scores).astype(BF16), preferred_element_type=F32)
 
-    def attend(slot, start, rows, sets, first=False):
-        for h in range(HEADS):
-            ext = values(slot, start, rows, h)
-            for q in sets:
-                o = weighted(slot, start, rows, h, ext, q, pl.ds(0, IMG))
-                if first:
-                    oacc[q, h] = o
-                else:
-                    oacc[q, h] += o
-
-    attend(z, 0, TOK, (0,), first=True)
-    z_first(1)
-    z_own(2)
+    def attend(slot, h, sets, start=0, rows=TOK, first=False):
+        ext = values(slot, start, rows, h)
+        for q in sets:
+            o = weighted(slot, start, rows, h, ext, q, pl.ds(0, IMG))
+            if first:
+                oacc[q, h] = o
+            else:
+                oacc[q, h] += o
+
+    def o_copy(h, at, k=0):
+        ref_at = (osend.at[h, :, at], orecv.at[h, :, at])
+        return remote(*ref_at, o_s.at[h + k], o_r.at[h + k], x_dev)
+
+    def pack(o, h, at):
+        den = o[HD : HD + 1]
+        high = den.astype(BF16).astype(F32)
+        middle = (den - high).astype(BF16).astype(F32)
+        low = den - high - middle
+        osend[h, pl.ds(0, HD), at] = o[:HD].astype(BF16)
+        pad = jnp.zeros((VROWS - HD - 3, den.shape[1]), F32)
+        osend[h, pl.ds(HD, VROWS - HD), at] = jnp.concatenate(
+            [high, middle, low, pad], axis=0
+        ).astype(BF16)
+
+    whole = pl.ds(0, IMG)
+
+    for h in range(HEADS):
+        attend(z, h, (0,), first=True)
+    z_first(3)
+    z_own(4)
     z_wait(0, 1)
     z_wait(0, 2)
+    z_wait(1, 1)
+    z_first(2)
+    z_own(5)
     for part in range(3):
         q_copy(part).wait_recv()
-    attend(z, 0, TOK, (1,), first=True)
-    for slot in (zm, zp, zo):
-        attend(slot, *PARTS[0], (1, 0))
-    z_wait(1, 1)
-    attend(zm, *PARTS[1], (1, 0))
-    attend(zp, *PARTS[1], (1, 0))
-    z_first(2)
+    for h in range(HEADS):
+        attend(z, h, (1,), first=True)
+    z_wait(2, 1)
+    attend(zm, 0, (1, 0))
+    attend(zp, 0, (1, 0))
+    z_first(4)
+    z_own(6)
+    z_wait(3, 1)
+    z_wait(4, 1)
+    attend(zm, 1, (1, 0))
     z_wait(1, 2)
-    attend(zo, *PARTS[1], (1, 0))
-    z_wait(2, 1)
-    attend(zm, *PARTS[2], (1, 0))
-    attend(zp, *PARTS[2], (1, 0))
     z_wait(2, 2)
+    attend(zo, 0, (1, 0))
+    pack(oacc[1, 0], 0, whole)
+    go(o_copy(0, whole))
+    z_first(5)
+    attend(zp, 1, (1, 0))
+    z_wait(3, 2)
+    z_wait(4, 2)
+    attend(zo, 1, (1, 0))
+    pack(oacc[1, 1], 1, whole)
+    go(o_copy(1, whole))
+    z_first(6)
+    z_wait(5, 1)
+    z_wait(6, 1)
+    attend(zm, 2, (1, 0))
+    attend(zp, 2, (1, 0))
+    z_wait(5, 2)
+    attend(zo, 2, (1, 0), 0, PARTS[2][0])
+    z_wait(6, 2)
 
     order = (yo, yp, ym, y)
-
-    def o_copy(j):
-        return remote(osend.at[j], orecv.at[j], o_s.at[j], o_r.at[j], x_dev)
 
     def lanes(i):
         return pl.ds(pl.multiple_of(i * 128, 128), 128)
 
-    last = [values(zo, *PARTS[2], h) for h in range(HEADS)]
+    last = values(zo, *PARTS[2], 2)
     for j in range(RING):
         at = lanes(order[j])
-        dens = []
-        for h in range(HEADS):
-            o = oacc[1, h, :, at] + weighted(zo, *PARTS[2], h, last[h], 1, at)
-            osend[j, pl.ds(h * HD, HD), :] = o[:HD].astype(BF16)
-            dens.append(o[HD : HD + 1])
-        whole = jnp.concatenate(dens, axis=0)
-        high = whole.astype(BF16)
-        rest = whole - high.astype(F32)
-        middle = rest.astype(BF16)
-        low = (rest - middle.astype(F32)).astype(BF16)
-        osend[j, pl.ds(FEAT, 16), :] = jnp.concatenate(
-            [high.astype(F32), middle.astype(F32), low.astype(F32), jnp.zeros((7, 128), F32)],
-            axis=0,
-        ).astype(BF16)
-        go(o_copy(j))
-    attend(zo, *PARTS[2], (0,))
+        pack(oacc[1, 2, :, at] + weighted(zo, *PARTS[2], 2, last, 1, at), 2, at)
+        go(o_copy(2, at, j))
+    attend(zo, 2, (0,), *PARTS[2])
+
+    for h in range(2):
+        o_copy(h, whole).wait_recv()
 
     def a_copy(j, columns):
         return remote(
@@ -496,14 +533,12 @@
 
     def combine(j):
         at = lanes(order[j])
-        o_copy(j).wait_recv()
-        tail = orecv[j, pl.ds(FEAT, 16), :].astype(F32)
+        o_copy(2, at, j).wait_recv()
         heads = []
         for h in range(HEADS):
-            num = oacc[0, h, pl.ds(0, HD), at] + orecv[j, pl.ds(h * HD, HD), :].astype(F32)
-            den = oacc[0, h, pl.ds(HD, 1), at] + (
-                tail[h : h + 1] + tail[3 + h : 4 + h] + tail[6 + h : 7 + h]
-            )
+            tail = orecv[h, pl.ds(HD, VROWS - HD), at].astype(F32)
+            num = oacc[0, h, pl.ds(0, HD), at] + orecv[h, pl.ds(0, HD), at].astype(F32)
+            den = oacc[0, h, pl.ds(HD, 1), at] + (tail[0:1] + tail[1:2] + tail[2:3])
             heads.append((num / den).T)
         atts[j] = jnp.concatenate(heads, axis=1).astype(BF16)
         go(a_copy(j, cols))
@@ -550,7 +585,8 @@
         p_copy(d, 2).wait_recv()
         pown[:, sides[d]] += racc[d].astype(F32)
 
-    rows = pl.ds(pl.multiple_of(TXT + t * CH, CH), CH)
+    row = t * CH + TXT * lax.min(lax.div(t * CH, HEAD_ROWS), 1)
+    rows = pl.ds(pl.multiple_of(row, CH), CH)
     resid = jnp.concatenate(
         [
             xg[i, rows, :].astype(F32)
@@ -596,13 +632,16 @@
     me = s * 8 + t
     rat[me] = jnp.broadcast_to(gap, (1, 128))
 
-    def tell(j, carry):
-        other = lax.rem(me + j, 64)
-        where = {"seq": lax.div(other, 8), "tensor": lax.rem(other, 8)}
+    def spot(step, here):
+        return lax.rem(here + step, RING)
+
+    seqs = [(1 - xlo if a else xlo) * RING + spot(b, z) for a in range(2) for b in range(RING)]
+    tens = [spot(b, y) * 2 + (1 - c if a else c) for a in range(2) for b in range(RING)]
+    hops = (0, 1, 2, 1, 1, 2, 3, 2)
+    pairs = [(i, j) for i in range(8) for j in range(8) if i or j]
+    for i, j in sorted(pairs, key=lambda p: -hops[p[0]] - hops[p[1]]):
+        where = {"seq": seqs[i], "tensor": tens[j]}
         remote(rat.at[me], rat.at[me], r_s.at[0], r_r.at[0], where).start()
-        return carry
-
-    lax.fori_loop(1, 64, tell, 0)
     told = rat.at[pl.ds(0, 63)]
     everyone = remote(told, told, r_s.at[0], r_r.at[0], mate)
     everyone.wait_recv()
@@ -639,8 +678,8 @@
     return pl.pallas_call(
         block,
         out_shape=(
-            jax.ShapeDtypeStruct(latent.shape, F32),
-            jax.ShapeDtypeStruct((1,), F32),
+            pltpu.VMEM(latent.shape, F32),
+            pltpu.SMEM((1,), F32),
         ),
         in_specs=[hbm] * 15,
         out_specs=(vmem, smem),
@@ -668,8 +707,8 @@
             pltpu.VMEM((2, IMG, FEAT), BF16),
             pltpu.VMEM((RING, TOK, PAIR), BF16),
             pltpu.VMEM((2, HEADS, VROWS, IMG), F32),
-            pltpu.VMEM((RING, FEAT + 16, 128), BF16),
-            pltpu.VMEM((RING, FEAT + 16, 128), BF16),
+            pltpu.VMEM((HEADS, VROWS, IMG), BF16),
+            pltpu.VMEM((HEADS, VROWS, IMG), BF16),
             pltpu.VMEM((RING, 128, FEAT), BF16),
             pltpu.VMEM((RING, CH, PAIR), BF16),
             pltpu.VMEM((2, CH, half), BF16),
@@ -680,7 +719,7 @@
             pltpu.VMEM((2, CH, half), BF16),
             pltpu.VMEM((2, CH, half), BF16),
             pltpu.VMEM((64, 1, 128), F32),
-            dma((19,)),
+            dma((20,)),
             dma((8,)),
             dma((8,)),
             dma((1,)),
@@ -689,12 +728,12 @@
             dma((2, 3, 3)),
             dma((2, 3, 3)),
             dma((2, 3, 3)),
-            dma((2, 3, 3)),
-            dma((2, 3, 3)),
+            dma((2, 7, 3)),
+            dma((2, 7, 3)),
             dma((3,)),
             dma((3,)),
-            dma((RING,)),
-            dma((RING,)),
+            dma((6,)),
+            dma((6,)),
             dma((RING,)),
             dma((RING,)),
             dma((1,)),

time: 84.9 us -> 80.6 us (0.949)
  Pallas kernels: 79.6 us -> 77.4 us
  between operations: 3.7 us -> 2.45 us
    pallas_call x1, Pallas kernels: 79.6 us -> 77.4 us  [shards(): pl.pallas_call(block, out_shape=(pltpu.VMEM(latent.shape, F32), pltpu.SME...]
where the time goes in v3:
time: 80.6 us; the launch traced here: 80.5 us
  Pallas kernels  77.4 us (96%)
  between operations  2.45 us (3%)
    pallas_call x1, Pallas kernels, shards(): pl.pallas_call(block, out_shape=(pltpu.VMEM(latent.shape, F32), pltpu.SME...  77.4 us

profile of v3, /device:TPU:1, one launch (start us, length us, event | category | flops | bytes accessed | tf_op | source)
XLA Modules:
  0.0 80.5 jit_solution(15685324535847466067)
XLA Ops:
  1.9 77.4 %shard_map.158 = (f32[1,64,64]{2,1,0:T(8,128)S(1)}, f32[1]{0:T(128)S(4)}) custom-call(s32[1]{0:T(128)S(6)} %copy.22.step_hbm, s32[1]{0:T(128)S(6)} %copy.21.group_hbm, s32[4]{0:T(128)} %length_hbm.1, bf16[1,512,384]{2,1,0:T(8,128)(2,1)} %x_hbm.1, bf16[4,64,384]{2,1,0:T(8,128)(2,1)} %text_hbm.1, bf16[3,3072,384]{2,1,0:T(8,128)(2,1)} %bitcast.5, ...), custom_call_target="tpu_custom_call" | custom-call | tf_op jit(solution)/shard_map/pallas_call | solution.py:678
  79.9 0.6 copy.19

commit v4 on v3

--- a/solution.py
+++ b/solution.py
@@ -19,8 +19,14 @@
 CH = 64
 RING = 4
 HEAD_ROWS = 128
-PARTS = ((0, 128), (128, 256), (384, 192))
-GROUPS = ((0, 0, 3),) + tuple((part, h, 1) for h in range(3) for part in (1, 2))
+PARTS = ((0, 128), (128, 192), (320, 256))
+EARLY = 96
+EARLY_AT = 320
+LATE_AT = EARLY_AT + EARLY
+EPARTS = ((0, 3 * EARLY),)
+ZPARTS = ((0, 128), (128, 192), (LATE_AT, TOK - LATE_AT))
+EPAD = 384
+GROUPS = ((0, 0, 3), (1, 0, 3), (2, 0, 1), (2, 1, 1), (2, 2, 1))
 VROWS = HD + 16
 PAD = 640
 
@@ -36,8 +42,8 @@
     )
 
 
-def piece(part, sub):
-    start, rows = PARTS[part]
+def piece(part, sub, parts=PARTS):
+    start, rows = parts[part]
     return pl.ds(start + sub * (rows // 2), rows // 2)
 
 
@@ -74,11 +80,15 @@
     old_ref,
     noise_ref,
     xg,
+    xe,
     modv,
     st_col,
     st_all,
+    st_early,
     stat,
+    stat_e,
     acc,
+    acc_e,
     qall,
     kv,
     oacc,
@@ -99,6 +109,10 @@
     st_r,
     own_s,
     own_r,
+    e_s,
+    e_r,
+    se_s,
+    se_r,
     y_s,
     y_r,
     l_s,
@@ -185,14 +199,19 @@
     x_load.wait()
     x_rest.wait()
 
-    mine = xg[y, :, cols].astype(F32)
-    part_mean = jnp.mean(mine, axis=-1, keepdims=True)
-    centred = mine - part_mean
-    part_sq = jnp.sum(centred * centred, axis=-1, keepdims=True)
-    lane = lax.broadcasted_iota(jnp.int32, (TOK, 128), 1)
-    st_col[pl.ds(0, TOK), :] = jnp.where(lane == 0, part_mean, jnp.where(lane == 1, part_sq, 0.0))
-    st_col[pl.ds(TOK, PAD - TOK), :] = jnp.zeros((PAD - TOK, 128), F32)
-    st_all[t] = st_col[...].T[0:2, :]
+    def shard_stats(mine, pad):
+        rows = mine.shape[0]
+        part_mean = jnp.mean(mine, axis=-1, keepdims=True)
+        centred = mine - part_mean
+        part_sq = jnp.sum(centred * centred, axis=-1, keepdims=True)
+        lane = lax.broadcasted_iota(jnp.int32, (rows, 128), 1)
+        st_col[pl.ds(0, rows), :] = jnp.where(
+            lane == 0, part_mean, jnp.where(lane == 1, part_sq, 0.0)
+        )
+        st_col[pl.ds(rows, pad - rows), :] = jnp.zeros((pad - rows, 128), F32)
+        return st_col[pl.ds(0, pad), :].T[0:2, :]
+
+    st_all[t] = shard_stats(xg[y, :, cols].astype(F32), PAD)
 
     pl.semaphore_wait(barrier, 14)
 
@@ -209,24 +228,29 @@
             return (y if sending else (ym, yp)[d]), (k if d == 0 else 1 - k)
         return ((ym, yp)[d] if sending else yo), d
 
+    def held(slot, part, sub, columns):
+        if part < 3:
+            return xg.at[slot, piece(part, sub), columns]
+        return xe.at[slot, piece(part - 3, sub, EPARTS), columns]
+
     def y_send(d, part, k):
         slot, sub = y_slot(d, k, True)
-        ref = xg.at[slot, piece(part, sub), cols]
+        ref = held(slot, part, sub, cols)
         return remote(ref, ref, y_s.at[d, part, k], y_r.at[d, part, k], y_dev[d])
 
     def y_arrival(d, part, k):
         slot, sub = y_slot(d, k, False)
-        ref = xg.at[slot, piece(part, sub), cols]
+        ref = held(slot, part, sub, cols)
         return remote(ref, ref, y_s.at[d, part, k], y_r.at[d, part, k], y_dev[d])
 
     def relay(d, part, k):
         slot, sub = y_slot(d, k, False)
-        ref = xg.at[slot, piece(part, sub), cols]
+        ref = held(slot, part, sub, cols)
         return remote(ref, ref, l_s.at[d, part, k], l_r.at[d, part, k], mate)
 
     def relay_arrival(d, part, k):
         slot, sub = y_slot(d, k, False)
-        ref = xg.at[slot, piece(part, sub), mate_cols]
+        ref = held(slot, part, sub, mate_cols)
         return remote(ref, ref, l_s.at[d, part, k], l_r.at[d, part, k], mate)
 
     def own_copy(columns):
@@ -239,14 +263,31 @@
         copy.start()
         sends.append(copy)
 
-    def y_own(part):
-        for k in range(2):
+    def y_own(part, pieces=(0, 1)):
+        for k in pieces:
             for d in range(2):
                 go(y_send(d, part, k))
 
     for j in range(1, 8):
         go(peer_copy(st_all, st_s, st_r, "tensor", t, j))
     y_own(0)
+
+    def early_copy(k):
+        to = (zp, zm, zo)[k]
+        return remote(
+            xg.at[y, pl.ds(EARLY_AT, EARLY), cols],
+            xe.at[y, pl.ds(k * EARLY, EARLY), cols],
+            e_s.at[k],
+            e_r.at[k],
+            {"seq": xlo * RING + to},
+        )
+
+    def early_mate(columns):
+        ref = xe.at[y, :, columns]
+        return remote(ref, ref, e_s.at[3], e_r.at[3], mate)
+
+    for k in range(3):
+        go(early_copy(k))
     go(own_copy(cols))
 
     def y_first(part):
@@ -274,18 +315,21 @@
     y_own(1)
     y_relay(0, 1)
 
+    def token_stats(buf, pad):
+        means = buf[:, 0, :]
+        squares = buf[:, 1, :]
+        mean = jnp.mean(means, axis=0, keepdims=True)
+        off = means - mean
+        total_sq = jnp.sum(squares, axis=0, keepdims=True) + FEAT * jnp.sum(
+            off * off, axis=0, keepdims=True
+        )
+        scale = lax.rsqrt(total_sq * (1.0 / WIDTH) + NORM_EPSILON)
+        sub_row = lax.broadcasted_iota(jnp.int32, (128, pad), 0)
+        return jnp.where(sub_row == 0, mean, jnp.where(sub_row == 1, scale, 0.0)).T
+
     for j in range(1, 8):
         peer_arrival(st_all, st_s, st_r, "tensor", t, j).wait_recv()
-    means = st_all[:, 0, :]
-    squares = st_all[:, 1, :]
-    mean = jnp.mean(means, axis=0, keepdims=True)
-    off = means - mean
-    total_sq = jnp.sum(squares, axis=0, keepdims=True) + FEAT * jnp.sum(
-        off * off, axis=0, keepdims=True
-    )
-    scale = lax.rsqrt(total_sq * (1.0 / WIDTH) + NORM_EPSILON)
-    sub_row = lax.broadcasted_iota(jnp.int32, (128, PAD), 0)
-    stat[...] = jnp.where(sub_row == 0, mean, jnp.where(sub_row == 1, scale, 0.0)).T
+    stat[...] = token_stats(st_all, PAD)
 
     for copy in loads:
         copy.wait()
@@ -309,6 +353,17 @@
             project_rows(slot, start, TXT, wt, 3, 4, first)
         else:
             project_rows(slot, start, rows, wi, 0, 1, first)
+
+    def project_early(slot, first=False):
+        at = pl.ds(*EPARTS[0])
+        n = (xe[slot, at, :].astype(F32) - stat_e[at, 0:1]) * stat_e[at, 1:2]
+        n = n * (1.0 + modv[slot, pl.ds(1, 1), :]) + modv[slot, pl.ds(0, 1), :]
+        w = wi[pl.ds(pl.multiple_of(slot * PAIR, 128), PAIR), pl.ds(FEAT, 2 * FEAT)]
+        p = jnp.dot(n.astype(BF16), w, preferred_element_type=F32)
+        if first:
+            acc_e[at, :] = p
+        else:
+            acc_e[at, :] += p
 
     score_scale = math.log2(math.e) / math.sqrt(HD)
 
@@ -337,6 +392,15 @@
                 q, qg_ref[...] * score_scale
             )
 
+    def finish_early(k):
+        slot = (zm, zp, zo)[k]
+        at = pl.ds(k * EARLY, EARLY)
+        to = pl.ds(EARLY_AT, EARLY)
+        for h in range(HEADS):
+            keys = acc_e[at, pl.ds(h * HD, HD)]
+            kv[slot, to, pl.ds(2 * h * HD, HD)] = head_norm(keys, kg_ref[...])
+            kv[slot, to, pl.ds((2 * h + 1) * HD, HD)] = acc_e[at, pl.ds(FEAT + h * HD, HD)].astype(BF16)
+
     def z_slot(d, k, sending):
         if k < 2:
             return (z if sending else (zm, zp)[d]), (k if d == 0 else 1 - k)
@@ -345,7 +409,7 @@
     def z_copy(d, g, k, sending):
         slot, sub = z_slot(d, k, sending)
         part, h, heads = GROUPS[g]
-        ref = kv.at[slot, piece(part, sub), pl.ds(2 * h * HD, 2 * heads * HD)]
+        ref = kv.at[slot, piece(part, sub, ZPARTS), pl.ds(2 * h * HD, 2 * heads * HD)]
         return remote(ref, ref, z_s.at[d, g, k], z_r.at[d, g, k], z_dev[d])
 
     def q_copy(part):
@@ -353,8 +417,8 @@
         at = pl.ds(query, rows)
         return remote(qall.at[0, at], qall.at[1, at], q_s.at[part], q_r.at[part], x_dev)
 
-    def z_own(g):
-        for k in range(2):
+    def z_own(g, pieces=(0, 1)):
+        for k in pieces:
             for d in range(2):
                 go(z_copy(d, g, k, True))
 
@@ -382,6 +446,12 @@
 
     y_first(1)
     y_own(2)
+    for k in range(3):
+        early_copy(k).wait_recv()
+    go(early_mate(cols))
+    st_early[t] = shard_stats(xe[y, :, cols].astype(F32), EPAD)
+    for j in range(1, 8):
+        go(peer_copy(st_early, se_s, se_r, "tensor", t, j))
     project(y, 1, first=True)
     y_relay(1, 1)
     y_ready(1, 0)
@@ -395,10 +465,10 @@
     project(yo, 1)
     finish(1)
     z_own(1)
-    z_own(3)
     go(q_copy(1))
 
     y_first(2)
+    y_own(3)
     y_relay(2, 1)
     y_ready(2, 0)
     y_ready(2, 1)
@@ -406,10 +476,17 @@
     project(yp, 2)
     z_first(1)
     y_relay(2, 2)
+    for j in range(1, 8):
+        peer_arrival(st_early, se_s, se_r, "tensor", t, j).wait_recv()
+    stat_e[...] = token_stats(st_early, EPAD)
+    early_mate(mate_cols).wait_recv()
+    project_early(y, first=True)
+    y_first(3)
     y_ready(2, 2)
     project(yo, 2)
     finish(2)
     z_own(2)
+    z_own(3, (0,))
     go(q_copy(2))
 
     for copy in late:
@@ -448,9 +525,15 @@
             else:
                 oacc[q, h] += o
 
-    def o_copy(h, at, k=0):
-        ref_at = (osend.at[h, :, at], orecv.at[h, :, at])
-        return remote(*ref_at, o_s.at[h + k], o_r.at[h + k], x_dev)
+    order = (yo, yp, ym, y)
+
+    def lanes(i):
+        return pl.ds(pl.multiple_of(i * 128, 128), 128)
+
+    def o_copy(h, j):
+        at = lanes(order[j])
+        k = h * RING + j
+        return remote(osend.at[h, :, at], orecv.at[h, :, at], o_s.at[k], o_r.at[k], x_dev)
 
     def pack(o, h, at):
         den = o[HD : HD + 1]
@@ -467,60 +550,70 @@
 
     for h in range(HEADS):
         attend(z, h, (0,), first=True)
-    z_first(3)
-    z_own(4)
+    y_relay(3, 1)
     z_wait(0, 1)
     z_wait(0, 2)
     z_wait(1, 1)
+    for h in range(HEADS):
+        attend(zm, h, (0,), 0, EARLY_AT)
+        attend(zp, h, (0,), 0, EARLY_AT)
+    z_wait(1, 2)
+    for h in range(HEADS):
+        attend(zo, h, (0,), 0, EARLY_AT)
     z_first(2)
-    z_own(5)
+    z_own(3, (1,))
+    z_own(4, (0,))
+    y_ready(3, 0)
+    y_ready(3, 1)
+    project_early(ym)
+    project_early(yp)
+    y_relay(3, 2)
+    z_first(3)
+    z_own(4, (1,))
     for part in range(3):
         q_copy(part).wait_recv()
     for h in range(HEADS):
         attend(z, h, (1,), first=True)
+    y_ready(3, 2)
+    project_early(yo)
+    for k in range(3):
+        finish_early(k)
     z_wait(2, 1)
-    attend(zm, 0, (1, 0))
-    attend(zp, 0, (1, 0))
+    attend(zm, 0, (1,))
+    attend(zp, 0, (1,))
     z_first(4)
-    z_own(6)
+    z_wait(2, 2)
+    attend(zo, 0, (1,))
+    pack(oacc[1, 0], 0, whole)
+    for j in range(3):
+        go(o_copy(0, j))
     z_wait(3, 1)
+    attend(zm, 1, (1,))
+    attend(zp, 1, (1,))
+    z_wait(3, 2)
+    attend(zo, 1, (1,))
+    pack(oacc[1, 1], 1, whole)
+    for j in range(2):
+        go(o_copy(1, j))
     z_wait(4, 1)
-    attend(zm, 1, (1, 0))
-    z_wait(1, 2)
-    z_wait(2, 2)
-    attend(zo, 0, (1, 0))
-    pack(oacc[1, 0], 0, whole)
-    go(o_copy(0, whole))
-    z_first(5)
-    attend(zp, 1, (1, 0))
-    z_wait(3, 2)
+    attend(zm, 2, (1,))
+    attend(zp, 2, (1,))
+    attend(zo, 2, (1,), 0, LATE_AT)
     z_wait(4, 2)
-    attend(zo, 1, (1, 0))
-    pack(oacc[1, 1], 1, whole)
-    go(o_copy(1, whole))
-    z_first(6)
-    z_wait(5, 1)
-    z_wait(6, 1)
-    attend(zm, 2, (1, 0))
-    attend(zp, 2, (1, 0))
-    z_wait(5, 2)
-    attend(zo, 2, (1, 0), 0, PARTS[2][0])
-    z_wait(6, 2)
-
-    order = (yo, yp, ym, y)
-
-    def lanes(i):
-        return pl.ds(pl.multiple_of(i * 128, 128), 128)
-
-    last = values(zo, *PARTS[2], 2)
+
+    last = values(zo, *ZPARTS[2], 2)
     for j in range(RING):
         at = lanes(order[j])
-        pack(oacc[1, 2, :, at] + weighted(zo, *PARTS[2], 2, last, 1, at), 2, at)
-        go(o_copy(2, at, j))
-    attend(zo, 2, (0,), *PARTS[2])
-
-    for h in range(2):
-        o_copy(h, whole).wait_recv()
+        pack(oacc[1, 2, :, at] + weighted(zo, *ZPARTS[2], 2, last, 1, at), 2, at)
+        go(o_copy(2, j))
+        if j == 1:
+            go(o_copy(1, 2))
+        if j == 2:
+            go(o_copy(0, 3))
+            go(o_copy(1, 3))
+    for h in range(HEADS):
+        for slot in (zm, zp, zo):
+            attend(slot, h, (0,), EARLY_AT, TOK - EARLY_AT)
 
     def a_copy(j, columns):
         return remote(
@@ -533,7 +626,8 @@
 
     def combine(j):
         at = lanes(order[j])
-        o_copy(2, at, j).wait_recv()
+        for h in range(HEADS):
+            o_copy(h, j).wait_recv()
         heads = []
         for h in range(HEADS):
             tail = orecv[h, pl.ds(HD, VROWS - HD), at].astype(F32)
@@ -699,11 +793,15 @@
             pltpu.VMEM((CH, CH), BF16),
             pltpu.VMEM((CH, CH), F32),
             pltpu.VMEM((RING, TOK, PAIR), BF16),
+            pltpu.VMEM((RING, 3 * EARLY, PAIR), BF16),
             pltpu.VMEM((RING, 8, PAIR), F32),
             pltpu.VMEM((PAD, 128), F32),
             pltpu.VMEM((8, 2, PAD), F32),
+            pltpu.VMEM((8, 2, EPAD), F32),
             pltpu.VMEM((PAD, 128), F32),
+            pltpu.VMEM((EPAD, 128), F32),
             pltpu.VMEM((TOK, 3 * FEAT), F32),
+            pltpu.VMEM((3 * EARLY, 2 * FEAT), F32),
             pltpu.VMEM((2, IMG, FEAT), BF16),
             pltpu.VMEM((RING, TOK, PAIR), BF16),
             pltpu.VMEM((2, HEADS, VROWS, IMG), F32),
@@ -724,16 +822,20 @@
             dma((8,)),
             dma((1,)),
             dma((1,)),
-            dma((2, 3, 3)),
-            dma((2, 3, 3)),
-            dma((2, 3, 3)),
-            dma((2, 3, 3)),
-            dma((2, 7, 3)),
-            dma((2, 7, 3)),
+            dma((4,)),
+            dma((4,)),
+            dma((8,)),
+            dma((8,)),
+            dma((2, 4, 3)),
+            dma((2, 4, 3)),
+            dma((2, 4, 3)),
+            dma((2, 4, 3)),
+            dma((2, 5, 3)),
+            dma((2, 5, 3)),
             dma((3,)),
             dma((3,)),
-            dma((6,)),
-            dma((6,)),
+            dma((12,)),
+            dma((12,)),
             dma((RING,)),
             dma((RING,)),
             dma((1,)),

time: 80.6 us -> 78.2 us (0.970)
  Pallas kernels: 77.4 us -> 75 us
    pallas_call x1, Pallas kernels: 77.4 us -> 75 us  [shards(): pl.pallas_call(block, out_shape=(pltpu.VMEM(latent.shape, F32), pltpu.SME...]
where the time goes in v4:
time: 78.2 us; the launch traced here: 78.1 us
  Pallas kernels  75 us (96%)
  between operations  2.45 us (3%)
    pallas_call x1, Pallas kernels, shards(): pl.pallas_call(block, out_shape=(pltpu.VMEM(latent.shape, F32), pltpu.SME...  75 us

profile of v4, /device:TPU:1, one launch (start us, length us, event | category | flops | bytes accessed | tf_op | source)
XLA Modules:
  0.0 78.1 jit_solution(11571047857963857350)
XLA Ops:
  1.9 75.0 %shard_map.158 = (f32[1,64,64]{2,1,0:T(8,128)S(1)}, f32[1]{0:T(128)S(4)}) custom-call(s32[1]{0:T(128)S(6)} %copy.22.step_hbm, s32[1]{0:T(128)S(6)} %copy.21.group_hbm, s32[4]{0:T(128)} %length_hbm.1, bf16[1,512,384]{2,1,0:T(8,128)(2,1)} %x_hbm.1, bf16[4,64,384]{2,1,0:T(8,128)(2,1)} %text_hbm.1, bf16[3,3072,384]{2,1,0:T(8,128)(2,1)} %bitcast.5, ...), custom_call_target="tpu_custom_call" | custom-call | tf_op jit(solution)/shard_map/pallas_call | solution.py:772
  77.5 0.6 copy.19

commit v5 on v4

--- a/solution.py
+++ b/solution.py
@@ -20,12 +20,12 @@
 RING = 4
 HEAD_ROWS = 128
 PARTS = ((0, 128), (128, 192), (320, 256))
-EARLY = 96
+EARLY = 64
 EARLY_AT = 320
 LATE_AT = EARLY_AT + EARLY
 EPARTS = ((0, 3 * EARLY),)
 ZPARTS = ((0, 128), (128, 192), (LATE_AT, TOK - LATE_AT))
-EPAD = 384
+EPAD = 256
 GROUPS = ((0, 0, 3), (1, 0, 3), (2, 0, 1), (2, 1, 1), (2, 2, 1))
 VROWS = HD + 16
 PAD = 640
@@ -486,7 +486,8 @@
     project(yo, 2)
     finish(2)
     z_own(2)
-    z_own(3, (0,))
+    z_own(3)
+    z_own(4, (0,))
     go(q_copy(2))
 
     for copy in late:
@@ -561,19 +562,18 @@
     for h in range(HEADS):
         attend(zo, h, (0,), 0, EARLY_AT)
     z_first(2)
-    z_own(3, (1,))
-    z_own(4, (0,))
+    z_own(4, (1,))
     y_ready(3, 0)
     y_ready(3, 1)
     project_early(ym)
     project_early(yp)
     y_relay(3, 2)
-    z_first(3)
-    z_own(4, (1,))
     for part in range(3):
         q_copy(part).wait_recv()
     for h in range(HEADS):
         attend(z, h, (1,), first=True)
+        if h == 1:
+            z_first(3)
     y_ready(3, 2)
     project_early(yo)
     for k in range(3):
@@ -662,16 +662,16 @@
             pown[:, sides[keep]] = out_side(j, keep)
 
     remote(my_wo, wo.at[pl.ds(pl.multiple_of((1 - c) * FEAT, 128), FEAT)], wo_s.at[0], wo_r.at[0], mate).wait_recv()
-    for j in range(RING):
+    for j in range(3):
         combine(j)
-        if j >= 1:
-            dispatch(j - 1)
-    a_copy(3, mate_cols).wait_recv()
-    mine = [out_side(3, d) for d in range(2)]
+        dispatch(j)
     for d in range(2):
         p_copy(d, 0).wait_recv()
         pacc[d] = (pown[:, sides[d]] + ropp[d].astype(F32)).astype(BF16)
         go(p_copy(d, 2))
+    combine(3)
+    a_copy(3, mate_cols).wait_recv()
+    mine = [out_side(3, d) for d in range(2)]
     for d in range(2):
         p_copy(1 - d, 1).wait_recv()
         pown[:, sides[d]] = mine[d] + rdir[1 - d].astype(F32)

time: 78.2 us -> 77.6 us (level)
  no operation moved by 1% of the time
where the time goes in v5:
time: 77.6 us; the launch traced here: 77.5 us
  Pallas kernels  74.4 us (96%)
  between operations  2.45 us (3%)
    pallas_call x1, Pallas kernels, shards(): pl.pallas_call(block, out_shape=(pltpu.VMEM(latent.shape, F32), pltpu.SME...  74.4 us

profile of v5, /device:TPU:1, one launch (start us, length us, event | category | flops | bytes accessed | tf_op | source)
XLA Modules:
  0.0 77.5 jit_solution(18230532350489687498)
XLA Ops:
  1.9 74.4 %shard_map.158 = (f32[1,64,64]{2,1,0:T(8,128)S(1)}, f32[1]{0:T(128)S(4)}) custom-call(s32[1]{0:T(128)S(6)} %copy.22.step_hbm, s32[1]{0:T(128)S(6)} %copy.21.group_hbm, s32[4]{0:T(128)} %length_hbm.1, bf16[1,512,384]{2,1,0:T(8,128)(2,1)} %x_hbm.1, bf16[4,64,384]{2,1,0:T(8,128)(2,1)} %text_hbm.1, bf16[3,3072,384]{2,1,0:T(8,128)(2,1)} %bitcast.5, ...), custom_call_target="tpu_custom_call" | custom-call | tf_op jit(solution)/shard_map/pallas_call | solution.py:772
  76.8 0.6 copy.19

commit v6 on v5

--- a/solution.py
+++ b/solution.py
@@ -582,14 +582,14 @@
     attend(zm, 0, (1,))
     attend(zp, 0, (1,))
     z_first(4)
+    z_wait(3, 1)
+    attend(zm, 1, (1,))
+    attend(zp, 1, (1,))
     z_wait(2, 2)
     attend(zo, 0, (1,))
     pack(oacc[1, 0], 0, whole)
     for j in range(3):
         go(o_copy(0, j))
-    z_wait(3, 1)
-    attend(zm, 1, (1,))
-    attend(zp, 1, (1,))
     z_wait(3, 2)
     attend(zo, 1, (1,))
     pack(oacc[1, 1], 1, whole)

time: 77.6 us -> 77.6 us (level)
  no operation moved by 1% of the time
where the time goes in v6:
time: 77.6 us; the launch traced here: 77.5 us
  Pallas kernels  74.4 us (96%)
  between operations  2.45 us (3%)
    pallas_call x1, Pallas kernels, shards(): pl.pallas_call(block, out_shape=(pltpu.VMEM(latent.shape, F32), pltpu.SME...  74.4 us

profile of v6, /device:TPU:1, one launch (start us, length us, event | category | flops | bytes accessed | tf_op | source)
XLA Modules:
  0.0 77.5 jit_solution(9840439199620157950)
XLA Ops:
  1.9 74.4 %shard_map.158 = (f32[1,64,64]{2,1,0:T(8,128)S(1)}, f32[1]{0:T(128)S(4)}) custom-call(s32[1]{0:T(128)S(6)} %copy.22.step_hbm, s32[1]{0:T(128)S(6)} %copy.21.group_hbm, s32[4]{0:T(128)} %length_hbm.1, bf16[1,512,384]{2,1,0:T(8,128)(2,1)} %x_hbm.1, bf16[4,64,384]{2,1,0:T(8,128)(2,1)} %text_hbm.1, bf16[3,3072,384]{2,1,0:T(8,128)(2,1)} %bitcast.5, ...), custom_call_target="tpu_custom_call" | custom-call | tf_op jit(solution)/shard_map/pallas_call | solution.py:772
  76.9 0.6 copy.19

commit v7 on v6

--- a/solution.py
+++ b/solution.py
@@ -590,13 +590,13 @@
     pack(oacc[1, 0], 0, whole)
     for j in range(3):
         go(o_copy(0, j))
+    z_wait(4, 1)
+    attend(zm, 2, (1,))
     z_wait(3, 2)
     attend(zo, 1, (1,))
     pack(oacc[1, 1], 1, whole)
     for j in range(2):
         go(o_copy(1, j))
-    z_wait(4, 1)
-    attend(zm, 2, (1,))
     attend(zp, 2, (1,))
     attend(zo, 2, (1,), 0, LATE_AT)
     z_wait(4, 2)

time: 77.6 us -> 77.6 us (level)
  no operation moved by 1% of the time
where the time goes in v7:
time: 77.6 us; the launch traced here: 77.5 us
  Pallas kernels  74.4 us (96%)
  between operations  2.45 us (3%)
    pallas_call x1, Pallas kernels, shards(): pl.pallas_call(block, out_shape=(pltpu.VMEM(latent.shape, F32), pltpu.SME...  74.4 us

profile of v7, /device:TPU:1, one launch (start us, length us, event | category | flops | bytes accessed | tf_op | source)
XLA Modules:
  0.0 77.5 jit_solution(338376706131351222)
XLA Ops:
  1.9 74.4 %shard_map.158 = (f32[1,64,64]{2,1,0:T(8,128)S(1)}, f32[1]{0:T(128)S(4)}) custom-call(s32[1]{0:T(128)S(6)} %copy.22.step_hbm, s32[1]{0:T(128)S(6)} %copy.21.group_hbm, s32[4]{0:T(128)} %length_hbm.1, bf16[1,512,384]{2,1,0:T(8,128)(2,1)} %x_hbm.1, bf16[4,64,384]{2,1,0:T(8,128)(2,1)} %text_hbm.1, bf16[3,3072,384]{2,1,0:T(8,128)(2,1)} %bitcast.5, ...), custom_call_target="tpu_custom_call" | custom-call | tf_op jit(solution)/shard_map/pallas_call | solution.py:772
  76.9 0.6 copy.19
